TPU v7x, 32 devices: a whole 2x2x4 slice. The times are simulated.
32 devices in a mesh: tok: 16 (over z, y, core), tp: 2 (over x).
Axes of the slice: x: 2, y: 2, z: 4, core: 2. Of those that a mesh axis runs over, the one named last changes fastest.
Arguments:
- hidden: bfloat16 [1536, 8192], P('tok'), may hold values from -2600 to 2600
- norm_gain: float32 [8192], replicated, may hold values from 0.5 to 1.5
- w_query: bfloat16 [8192, 4096], P('tok', 'tp'), may hold values from -1 to 1
- w_key: bfloat16 [8192, 1024], P('tok', 'tp'), may hold values from -1 to 1
- w_value: bfloat16 [8192, 1024], P('tok', 'tp'), may hold values from -0.0625 to 0.0625
- doc_ids: int32 [1536], P('tok'), may hold values from 0 to 3, as said below
Outputs:
- attended: bfloat16 [1536, 4096], P('tok', 'tp')
- out_scale: float32 [4096], P('tp')
- folded_gain: float32 [8192], P(('tok', 'tp'))
- codes_query: float32 [8192, 4096], P(('tok', 'tp'))
- codes_key: float32 [8192, 1024], P(('tok', 'tp'))
- codes_value: float32 [8192, 1024], P(('tok', 'tp'))
- scale_query: float32 [4096], P('tp')
- scale_key: float32 [1024], P('tp')
- scale_value: float32 [1024], P('tp')
Inputs may be any that keep to these rules, and one draw needn't show every extreme that they name: doc_ids never falls along the tokens; each of the 4 documents holds 1 to 1152 tokens and one holds exactly 1152.
All inputs are finite; a program needn't handle non-finite values. Where the computation divides by a largest or mean magnitude, that divisor is 1e-20 or more.
Results may differ from a plain program's by a relative error of at most 0.005.
The roundings to bfloat16 on the way count: a program that leaves them out, or rounds other values in their place, can miss the bound.
Values may be sent and summed in bfloat16 or wider, within the bound.
A program may use at most 128 MiB of HBM per device.

v0:
```python
import functools
import math

import jax
import jax.numpy as jnp
from jax import lax
from jax.experimental import pallas as pl
from jax.experimental.pallas import tpu as pltpu
from jax.sharding import PartitionSpec as P

HEAD = 128
KVH = 8
QHEADS = 32


def rotation(positions):
    half = HEAD // 2
    inverse = jnp.exp(
        jnp.arange(half, dtype=jnp.float32) * (-2.0 * math.log(10000.0) / HEAD)
    )
    angles = positions[:, None] * inverse[None, :]
    cosine, sine = jnp.cos(angles), jnp.sin(angles)
    return (
        jnp.concatenate([cosine, cosine], axis=1),
        jnp.concatenate([-sine, sine], axis=1),
    )


def smooth_from(input_peak, weight_peak):
    return jnp.sqrt(jnp.maximum(input_peak, 1e-05)) / jnp.sqrt(jnp.maximum(weight_peak, 1e-05))


MESH = pl.DeviceIdType.MESH
QUAD = 4


def column_chunks(widths, most=512):
    return [
        (which, start, min(most, width - start))
        for which, width in enumerate(widths)
        for start in range(0, width, most)
    ]


def meet_all(barrier, me, tp, tok_count, tp_count):
    def greet(step, carry):
        other = lax.rem(me + step, tok_count)
        pl.semaphore_signal(barrier, inc=1, device_id=(other, tp), device_id_type=MESH)
        return carry

    lax.fori_loop(1, tok_count, greet, 0)
    for step in range(1, tp_count):
        other = lax.rem(tp + step, tp_count)
        pl.semaphore_signal(barrier, inc=1, device_id=(me, other), device_id_type=MESH)
    pl.semaphore_wait(barrier, tok_count - 1 + tp_count - 1)


def front_kernel(
    chunks,
    line,
    tp_count,
    share,
    normed_ref,
    doc_ref,
    cosine_ref,
    sine_ref,
    wq_ref,
    wk_ref,
    wv_ref,
    query_ref,
    kv_ref,
    peak_ref,
    docs_ref,
    rq_ref,
    rk_ref,
    rv_ref,
    mine,
    theirs,
    held_q,
    held_k,
    held_v,
    tokens,
    partial,
    from_left,
    from_right,
    w_send,
    w_recv,
    t_send,
    t_recv,
    m_send,
    m_recv,
    x_send,
    x_recv,
    x_local,
    r_send,
    r_recv,
    l_send,
    l_recv,
    p_send,
    p_recv,
    d_send,
    d_recv,
):
    me = lax.axis_index("tok")
    tp = lax.axis_index("tp")
    quad = lax.rem(me, QUAD)
    place = me // QUAD
    rows = wq_ref.shape[0]
    tok_dev = normed_ref.shape[0]
    sib = me + 1 - 2 * lax.rem(me, 2)
    side = me + 2 - 4 * (quad // 2)
    side_sib = side + 1 - 2 * lax.rem(me, 2)
    own = (wq_ref, wk_ref, wv_ref)
    held = (held_q, held_k, held_v)
    relaid = (rq_ref, rk_ref, rv_ref)
    sub = rows // tp_count

    def remote(src, dst, send, recv, tok, tp_to=None):
        return pltpu.make_async_remote_copy(
            src_ref=src,
            dst_ref=dst,
            send_sem=send,
            recv_sem=recv,
            device_id=(tok, tp if tp_to is None else tp_to),
            device_id_type=MESH,
        )

    barrier = pltpu.get_barrier_semaphore()
    meet_all(barrier, me, tp, line * QUAD, tp_count)

    def w_copy(kind, c):
        which, start, width = chunks[c]
        cols = pl.ds(start, width)
        if kind == 2:
            src = held[which].at[1, :, cols]
        else:
            src = own[which].at[:, cols]
        return remote(
            src,
            held[which].at[kind, :, cols],
            w_send.at[kind, c],
            w_recv.at[kind, c],
            side if kind == 1 else sib,
        )

    part = tok_dev // share
    piece = lax.rem(tp, share)
    mate = tp + 1 - 2 * piece

    def t_copy(step):
        to = lax.rem(place + step, line)
        width = QUAD * rows
        first = pl.multiple_of(piece * part, 16)
        return remote(
            normed_ref.at[
                pl.ds(first, part), pl.ds(pl.multiple_of(to * width, 128), width)
            ],
            tokens.at[pl.ds(pl.multiple_of(place * tok_dev + first, 16), part)],
            t_send.at[step],
            t_recv.at[step],
            to * QUAD + quad,
        )

    def m_copy(step):
        source = lax.rem(place - step + line, line)
        first = pl.multiple_of(source * tok_dev + piece * part, 16)
        got = tokens.at[pl.ds(first, part)]
        return remote(got, got, m_send.at[step], m_recv.at[step], me, mate)

    def x_copy(which, step):
        to = lax.rem(tp + step, tp_count)
        width = own[which].shape[1]
        src = own[which].at[pl.ds(pl.multiple_of(to * sub, 16), sub)]
        dst = relaid[which].at[:, pl.ds(pl.multiple_of(tp * width, 128), width)]
        if step == 0:
            return pltpu.make_async_copy(src, dst, x_local.at[which])
        return remote(src, dst, x_send.at[which, step], x_recv.at[which, step], me, to)

    def d_copy(step):
        return remote(
            doc_ref,
            docs_ref.at[me],
            d_send.at[step],
            d_recv.at[step],
            lax.rem(me + step, line * QUAD),
        )

    def p_copy(kind):
        return remote(
            mine,
            theirs.at[kind],
            p_send.at[kind],
            p_recv.at[kind],
            (sib, side, side_sib)[kind],
        )

    def d_start(step, carry):
        d_copy(step).start()
        return carry

    def d_wait(step, carry):
        d_copy(step).wait()
        return carry

    for step in range(1, line):
        t_copy(step).start()
    for c in range(len(chunks)):
        w_copy(1, c).start()
        w_copy(0, c).start()
    width = QUAD * rows
    tokens[pl.ds(pl.multiple_of(place * tok_dev, 16), tok_dev)] = normed_ref[
        :, pl.ds(pl.multiple_of(place * width, 128), width)
    ]
    for step in range(1, line):
        t_copy(step).wait_recv()
        if share == 2:
            m_copy(step).start()
    for which in range(3):
        for step in range(tp_count):
            x_copy(which, step).start()
    if share == 2:
        for step in range(1, line):
            m_copy(step).wait_recv()
    mine[...] = jnp.max(
        jnp.abs(tokens[...].astype(jnp.float32)), axis=0, keepdims=True
    )
    docs_ref[me] = doc_ref[...]
    lax.fori_loop(1, line * QUAD, d_start, 0)

    def span(c):
        which, start, size = chunks[c]
        base = sum(own[i].shape[1] for i in range(which)) + start
        return slice(base, base + size)

    def block(d):
        return pl.ds(pl.multiple_of(d * tok_dev, 8), tok_dev)

    def right(c, d):
        cols = span(c)
        return remote(
            partial.at[block(d), cols],
            from_left.at[block(d), cols],
            r_send.at[c, d],
            r_recv.at[c, d],
            me + QUAD,
        )

    def left(c, d):
        cols = span(c)
        return remote(
            partial.at[block(d), cols],
            from_right.at[block(d), cols],
            l_send.at[c, d],
            l_recv.at[c, d],
            me - QUAD,
        )

    def add_left(c, d):
        right(c, d).wait_recv()
        cols = span(c)
        partial[block(d), cols] = partial[block(d), cols] + from_left[block(d), cols]

    def add_right(c, d):
        left(c, d).wait_recv()
        cols = span(c)
        partial[block(d), cols] = partial[block(d), cols] + from_right[block(d), cols]

    def first_sends(c):
        @pl.when(place == 0)
        def _():
            def go(i, carry):
                right(c, line - 1 - i).start()
                return carry

            lax.fori_loop(0, line - 1, go, 0)

        @pl.when(place == line - 1)
        def _():
            def go(i, carry):
                left(c, i).start()
                return carry

            lax.fori_loop(0, line - 1, go, 0)

    def reduce(c):
        def go(i, carry):
            to_right = line - 1 - i

            @pl.when((place > 0) & (to_right > place))
            def _():
                add_left(c, to_right)
                right(c, to_right).start()

            @pl.when((place < line - 1) & (i < place))
            def _():
                add_right(c, i)
                left(c, i).start()

            return carry

        lax.fori_loop(0, line, go, 0)

    def finish(c):
        @pl.when(place > 0)
        def _():
            add_left(c, place)

        @pl.when(place < line - 1)
        def _():
            add_right(c, place)

        which, start, size = chunks[c]
        for head in range(size // HEAD):
            base = span(c).start + head * HEAD
            states = partial[block(place), base : base + HEAD]
            if which < 2:
                states = (
                    states * cosine_ref[...]
                    + pltpu.roll(states, HEAD // 2, 1) * sine_ref[...]
                )
            at = start + head * HEAD + (wk_ref.shape[1] if which == 2 else 0)
            target = query_ref if which == 0 else kv_ref
            target[:, at : at + HEAD] = states.astype(jnp.bfloat16)

    def columns_of(tok):
        return pl.ds(pl.multiple_of(lax.rem(tok, QUAD) * rows, 128), rows)

    for c in range(len(chunks)):
        which, start, size = chunks[c]
        cols = slice(start, start + size)
        w_copy(1, c).wait_recv()
        w_copy(2, c).start()
        total = jnp.dot(
            tokens[:, columns_of(me)],
            own[which][:, cols],
            preferred_element_type=jnp.float32,
        )
        total += jnp.dot(
            tokens[:, columns_of(side)],
            held[which][1, :, cols],
            preferred_element_type=jnp.float32,
        )
        w_copy(0, c).wait_recv()
        total += jnp.dot(
            tokens[:, columns_of(sib)],
            held[which][0, :, cols],
            preferred_element_type=jnp.float32,
        )
        w_copy(2, c).wait_recv()
        total += jnp.dot(
            tokens[:, columns_of(side_sib)],
            held[which][2, :, cols],
            preferred_element_type=jnp.float32,
        )
        partial[:, span(c)] = total
        first_sends(c)
        if c == 0:
            for kind in range(3):
                p_copy(kind).start()
        if c > 0:
            reduce(c - 1)
    reduce(len(chunks) - 1)
    for c in range(len(chunks)):
        finish(c)

    for kind in range(3):
        p_copy(kind).wait()
    peak_ref[...] = jnp.maximum(
        jnp.maximum(mine[...], theirs[0]), jnp.maximum(theirs[1], theirs[2])
    )
    lax.fori_loop(1, line * QUAD, d_wait, 0)
    for step in range(1, line):
        t_copy(step).wait_send()
        if share == 2:
            m_copy(step).wait_send()
    for c in range(len(chunks)):
        for kind in range(3):
            w_copy(kind, c).wait_send()

        def sent(d, carry):
            @pl.when(d > place)
            def _():
                right(c, d).wait_send()

            @pl.when(d < place)
            def _():
                left(c, d).wait_send()

            return carry

        lax.fori_loop(0, line, sent, 0)
    for which in range(3):
        x_copy(which, 0).wait()
        for step in range(1, tp_count):
            x_copy(which, step).wait_send()
            x_copy(which, step).wait_recv()


def front(normed, doc_row, cosine, sine, matrices):
    tok_count, tp_count = lax.axis_size("tok"), lax.axis_size("tp")
    line = tok_count // QUAD
    tok_dev = normed.shape[0]
    rows = matrices[0].shape[0]
    widths = [matrix.shape[1] for matrix in matrices]
    chunks = column_chunks(widths)
    total = sum(widths)
    share = 2 if tp_count % 2 == 0 and tok_dev % 32 == 0 else 1
    vmem = pl.BlockSpec(memory_space=pltpu.VMEM)
    dma = pltpu.SemaphoreType.DMA
    return pl.pallas_call(
        functools.partial(front_kernel, chunks, line, tp_count, share),
        out_shape=(
            jax.ShapeDtypeStruct((tok_dev, widths[0]), jnp.bfloat16),
            jax.ShapeDtypeStruct((tok_dev, widths[1] + widths[2]), jnp.bfloat16),
            jax.ShapeDtypeStruct((1, QUAD * rows), jnp.float32),
            jax.ShapeDtypeStruct((tok_count,) + doc_row.shape, jnp.int32),
        )
        + tuple(
            jax.ShapeDtypeStruct((rows // tp_count, width * tp_count), jnp.bfloat16)
            for width in widths
        ),
        in_specs=[vmem] * 7,
        out_specs=(vmem,) * 4 + (pl.BlockSpec(memory_space=pl.ANY),) * 3,
        scratch_shapes=[
            pltpu.VMEM((1, QUAD * rows), jnp.float32),
            pltpu.VMEM((3, 1, QUAD * rows), jnp.float32),
        ]
        + [
            pltpu.VMEM((3, rows, width), jnp.bfloat16) for width in widths
        ]
        + [
            pltpu.VMEM((line * tok_dev, QUAD * rows), jnp.bfloat16),
            pltpu.VMEM((line * tok_dev, total), jnp.float32),
            pltpu.VMEM((line * tok_dev, total), jnp.float32),
            pltpu.VMEM((line * tok_dev, total), jnp.float32),
            dma((3, len(chunks))),
            dma((3, len(chunks))),
            dma((line,)),
            dma((line,)),
            dma((line,)),
            dma((line,)),
            dma((3, tp_count)),
            dma((3, tp_count)),
            dma((3,)),
            dma((len(chunks), line)),
            dma((len(chunks), line)),
            dma((len(chunks), line)),
            dma((len(chunks), line)),
            dma((3,)),
            dma((3,)),
            dma((tok_count,)),
            dma((tok_count,)),
        ],
        compiler_params=pltpu.CompilerParams(
            collective_id=0, has_side_effects=True, vmem_limit_bytes=60 * 1024 * 1024
        ),
    )(normed, doc_row, cosine, sine, *matrices)


def back_kernel(
    line,
    tp_count,
    kv_here,
    query_ref,
    kv_ref,
    doc_mine_ref,
    doc_all_ref,
    column_ref,
    out_ref,
    out_peak_ref,
    scale_ref,
    cache,
    column_tp,
    column_mid,
    column_all,
    out_mine,
    out_all,
    z_send,
    z_recv,
    y_send,
    y_recv,
    s_send,
    s_recv,
    c_send,
    c_recv,
    a_send,
    a_recv,
    o_send,
    o_recv,
):
    me = lax.axis_index("tok")
    tp = lax.axis_index("tp")
    tok_count = line * QUAD
    quad = lax.rem(me, QUAD)
    place = me // QUAD
    tok_dev = query_ref.shape[0]
    keys = cache.shape[0]
    sib = me + 1 - 2 * lax.rem(me, 2)
    side = me + 2 - 4 * (quad // 2)

    def remote(src, dst, send, recv, tok, tp_to=None):
        return pltpu.make_async_remote_copy(
            src_ref=src,
            dst_ref=dst,
            send_sem=send,
            recv_sem=recv,
            device_id=(tok, tp if tp_to is None else tp_to),
            device_id_type=MESH,
        )

    def rows_of(tok):
        return pl.ds(pl.multiple_of(tok * tok_dev, 16), tok_dev)

    def z_copy(step):
        to = lax.rem(place + step, line) * QUAD + quad
        return remote(
            kv_ref, cache.at[rows_of(me)], z_send.at[step], z_recv.at[step], to
        )

    def line_source(step):
        return lax.rem(place - step + line, line) * QUAD

    def y_copy(step):
        tok = line_source(step) + quad
        src = kv_ref if step == 0 else cache.at[rows_of(tok)]
        return remote(
            src, cache.at[rows_of(tok)], y_send.at[step], y_recv.at[step], side
        )

    def s_copy(step, of_side):
        tok = line_source(step) + (lax.rem(side, QUAD) if of_side else quad)
        src = kv_ref if step == 0 and not of_side else cache.at[rows_of(tok)]
        slot = step + (line if of_side else 0)
        return remote(src, cache.at[rows_of(tok)], s_send.at[slot], s_recv.at[slot], sib)

    def c_copy(step):
        return remote(
            column_ref,
            column_tp.at[step],
            c_send.at[step],
            c_recv.at[step],
            me,
            lax.rem(tp + step, tp_count),
        )

    def a_copy(step):
        return remote(
            column_mid,
            column_all.at[me],
            a_send.at[step],
            a_recv.at[step],
            lax.rem(me + step, tok_count),
        )

    def o_copy(step):
        return remote(
            out_mine,
            out_all.at[me],
            o_send.at[step],
            o_recv.at[step],
            lax.rem(me + step, tok_count),
        )

    def each(copy, act):
        def go(step, carry):
            getattr(copy(step), act)()
            return carry

        lax.fori_loop(1, tok_count, go, 0)

    meet_all(pltpu.get_barrier_semaphore(), me, tp, tok_count, tp_count)
    for step in range(1, tp_count):
        c_copy(step).start()
    y_copy(0).start()
    for step in range(1, line):
        z_copy(step).start()
    s_copy(0, False).start()
    cache[rows_of(me)] = kv_ref[...]
    joined = column_ref[...]
    for step in range(1, tp_count):
        c_copy(step).wait()
        joined = jnp.maximum(joined, column_tp[step])
    column_mid[...] = joined
    column_all[me] = joined
    for step in range(1, line):
        z_copy(step).wait_recv()
        y_copy(step).start()
        s_copy(step, False).start()
    for step in range(line):
        y_copy(step).wait_recv()
        s_copy(step, True).start()
    for step in range(line):
        s_copy(step, False).wait_recv()
        s_copy(step, True).wait_recv()

    each(a_copy, "start")
    position = lax.broadcasted_iota(jnp.int32, (tok_dev, keys), 0) + me * tok_dev
    allowed = (doc_mine_ref[...] == doc_all_ref[...]) & (
        lax.broadcasted_iota(jnp.int32, (tok_dev, keys), 1) <= position
    )
    group = QHEADS // KVH
    for kv in range(kv_here):
        heads = [
            slice((kv * group + g) * HEAD, (kv * group + g + 1) * HEAD)
            for g in range(group)
        ]
        query = jnp.concatenate([query_ref[:, head] for head in heads], axis=0)
        key = cache[:, kv * HEAD : (kv + 1) * HEAD]
        value = cache[:, (kv_here + kv) * HEAD : (kv_here + kv + 1) * HEAD]
        scores = lax.dot_general(
            query, key, (((1,), (1,)), ((), ())), preferred_element_type=jnp.float32
        ) * (1.0 / math.sqrt(HEAD))
        scores = jnp.where(
            allowed[None], scores.reshape(group, tok_dev, keys), -1e30
        ).reshape(group * tok_dev, keys)
        weights = jnp.exp(scores - jnp.max(scores, axis=1, keepdims=True))
        totals = jnp.sum(weights, axis=1, keepdims=True)
        mixed = jnp.dot(
            weights.astype(jnp.bfloat16), value, preferred_element_type=jnp.float32
        )
        mixed = (mixed / totals).astype(jnp.bfloat16)
        for g, head in enumerate(heads):
            piece = mixed[g * tok_dev : (g + 1) * tok_dev]
            out_ref[:, head] = piece
            out_mine[:, head] = jnp.max(
                jnp.abs(piece.astype(jnp.float32)), axis=0, keepdims=True
            )
    out_all[me] = out_mine[...]
    each(o_copy, "start")
    each(a_copy, "wait")
    scale_ref[...] = jnp.maximum(jnp.max(column_all[...], axis=0), 1e-05) / 127.0
    each(o_copy, "wait")
    out_peak_ref[...] = jnp.max(out_all[...], axis=0)
    for step in range(line):
        if step > 0:
            z_copy(step).wait_send()
        y_copy(step).wait_send()
        s_copy(step, False).wait_send()
        s_copy(step, True).wait_send()


def back(query, keys_values, doc_mine, doc_all, column_local):
    tok_count, tp_count = lax.axis_size("tok"), lax.axis_size("tp")
    line = tok_count // QUAD
    tok_dev, width = query.shape
    kv_here = keys_values.shape[1] // (2 * HEAD)
    columns = column_local.shape[1]
    vmem = pl.BlockSpec(memory_space=pltpu.VMEM)
    dma = pltpu.SemaphoreType.DMA
    f32 = jnp.float32
    return pl.pallas_call(
        functools.partial(back_kernel, line, tp_count, kv_here),
        out_shape=(
            jax.ShapeDtypeStruct((tok_dev, width), jnp.bfloat16),
            jax.ShapeDtypeStruct((1, width), f32),
            jax.ShapeDtypeStruct((1, columns), f32),
        ),
        in_specs=[vmem] * 5,
        out_specs=(vmem,) * 3,
        scratch_shapes=[
            pltpu.VMEM((tok_dev * tok_count, keys_values.shape[1]), jnp.bfloat16),
            pltpu.VMEM((tp_count, 1, columns), f32),
            pltpu.VMEM((1, columns), f32),
            pltpu.VMEM((tok_count, 1, columns), f32),
            pltpu.VMEM((1, width), f32),
            pltpu.VMEM((tok_count, 1, width), f32),
        ]
        + [dma((line,))] * 4
        + [dma((2 * line,))] * 2
        + [dma((tp_count,))] * 2
        + [dma((tok_count,))] * 4,
        compiler_params=pltpu.CompilerParams(
            collective_id=1, has_side_effects=True, vmem_limit_bytes=60 * 1024 * 1024
        ),
    )(query, keys_values, doc_mine, doc_all, column_local)


def on_device(hidden, norm_gain, w_query, w_key, w_value, doc_ids):
    tok_dev = hidden.shape[0]
    row_count = w_query.shape[0]
    tp_count = lax.axis_size("tp")
    tok_index = lax.axis_index("tok")
    tp_index = lax.axis_index("tp")
    matrices = (w_query, w_key, w_value)
    states = hidden.astype(jnp.float32)
    normed = (
        states
        * lax.rsqrt(jnp.mean(states * states, axis=1, keepdims=True) + 1e-05)
        * norm_gain[None, :]
    ).astype(jnp.bfloat16)
    lanes = -tok_dev % 128
    doc_row = jnp.pad(doc_ids, (0, lanes))[None]
    positions = (tok_index * tok_dev + jnp.arange(tok_dev, dtype=jnp.int32)).astype(
        jnp.float32
    )
    query, keys_values, peaks, docs, *relaid = front(
        normed, doc_row, *rotation(positions), matrices
    )
    doc_all = docs[:, 0, :tok_dev].reshape(1, -1)
    sub_rows = row_count // tp_count
    smooth_part = smooth_from(
        lax.dynamic_slice_in_dim(
            peaks[0], (tok_index % QUAD) * row_count + tp_index * sub_rows, sub_rows
        ),
        functools.reduce(
            jnp.maximum, [jnp.max(jnp.abs(block), axis=1) for block in relaid]
        ).astype(jnp.float32),
    )
    column_local = jnp.concatenate(
        [
            jnp.max(jnp.abs(smooth_part[:, None] * block.astype(jnp.float32)), axis=0)
            for block in relaid
        ]
    )
    attended, out_scale, column_scales = back(
        query,
        keys_values,
        doc_ids[:, None],
        doc_all,
        column_local[None],
    )
    out_scale = out_scale[0]
    every = column_scales[0]
    every_scale = jnp.split(
        every, [relaid[0].shape[1], relaid[0].shape[1] + relaid[1].shape[1]]
    )
    scales = tuple(
        lax.dynamic_slice_in_dim(scale, tp_index * matrix.shape[1], matrix.shape[1])
        for scale, matrix in zip(every_scale, matrices)
    )
    gain_part = lax.dynamic_slice_in_dim(
        norm_gain, tok_index * row_count + tp_index * sub_rows, sub_rows
    )
    folded_gain = gain_part / smooth_part
    codes = tuple(
        (
            smooth_part[:, None] * block.astype(jnp.float32) / column_scale[None, :]
            for block, column_scale in zip(relaid, every_scale)
        )
    )
    return (
        attended,
        out_scale,
        folded_gain,
        codes[0],
        codes[1],
        codes[2],
        scales[0],
        scales[1],
        scales[2],
    )


def solution(mesh):
    in_specs = (P("tok", None), P(), P("tok", "tp"), P("tok", "tp"), P("tok", "tp"), P("tok"))
    out_specs = (
        P("tok", "tp"),
        P("tp"),
        P(("tok", "tp")),
        P(("tok", "tp"), None),
        P(("tok", "tp"), None),
        P(("tok", "tp"), None),
        P("tp"),
        P("tp"),
        P("tp"),
    )
    return jax.shard_map(
        on_device, mesh=mesh, in_specs=in_specs, out_specs=out_specs, check_vma=False
    )
```

profile of v0, /device:TPU:0, one launch (start us, length us, event | category | flops | bytes accessed | tf_op | source)
XLA Modules:
  0.0 213.9 jit_solution(10127324713648564669)
XLA Ops:
  0.6 0.0 copy-start.5
  0.7 1.8 fusion.1
  2.5 3.0 %fusion.3.normed_ref = bf16[96,8192]{1,0:T(8,128)(2,1)} fusion(bf16[96,8192]{1,0:T(8,128)(2,1)} %param.6, f32[8192]{0:T(1024)} %param.7, f32[96]{0:T(128)S(1)} %add_rsqrt_fusion), kind=kLoop, calls=%fused_computation.7 | loop fusion | flops 3145728 | bytes 3178880 | tf_op jit(solution)/shard_map/convert_element_type | solution.py:690
  5.5 0.5 pad_bitcast_fusion.doc_ref
  6.0 0.3 fusion.6
  6.3 0.7 pad_maximum_fusion
  7.0 141.6 %shard_map.133 = (bf16[96,2048]{1,0:T(8,128)(2,1)}, bf16[96,1024]{1,0:T(8,128)(2,1)}, f32[1,2048]{1,0:T(1,128)}, s32[16,1,128]{2,1,0:T(1,128)}, bf16[256,4096]{1...) custom-call(bf16[96,8192]{1,0:T(8,128)(2,1)} %fusion.3.normed_ref, ...), custom_call_target="tpu_custom_call" | custom-call | tf_op jit(solution)/shard_map/pallas_call | solution.py:410
  148.6 0.0 copy-start.1
  148.6 0.0 copy-start.2
  148.6 0.0 copy-start
  148.7 0.7 copy.15.doc_mine_ref
  149.4 0.9 slice_reduce_fusion
  150.3 0.7 reshape_squeeze.3.doc_all_ref
  151.0 0.7 maximum_sqrt_fusion
  151.7 1.2 abs_reduce_fusion.4
  152.9 2.1 abs_reduce_fusion.1
  154.9 1.2 abs_reduce_fusion.5
  156.2 1.3 dynamic-slice_divide_fusion
  157.5 0.0 copy-done.1
  157.5 0.3 abs_reduce_fusion.3
  157.8 0.5 abs_reduce_fusion
  158.3 0.6 pad_maximum_fusion.2
  158.9 46.1 %shard_map.134 = (bf16[96,2048]{1,0:T(8,128)(2,1)}, f32[1,2048]{1,0:T(1,128)}, f32[1,6144]{1,0:T(1,128)}) custom-call(bf16[96,2048]{1,0:T(8,128)(2,1)} %get-tuple-element.19.query_ref, bf16[96,1024]{1,0:T(8,128)(2,1)} %get-tuple-element.20.kv_ref, s32[96,1]{1,0:T(8,128)} %copy.15.doc_mine_ref, s32[1,1536]{1,0:T(1,128)} %reshape_squeeze.3.doc_all_ref, ...), custom_call_target="tpu_custom_call" | custom-call | tf_op jit(solution)/shard_map/pallas_call | solution.py:651
  205.0 0.7 split.9
  205.8 2.7 %fusion = f32[256,4096]{1,0:T(8,128)} fusion(bf16[256,4096]{1,0:T(8,128)(2,1)S(1)} %copy-done, f32[4096]{0:T(1024)S(1)} %bitcast.12, f32[256]{0:T(256)S(1)} %get-tuple-element.32), kind=kLoop, calls=%fused_computation.2 | loop fusion | flops 3145728 | bytes 6308864 | tf_op jit(solution)/shard_map/div | solution.py:737
  208.5 0.7 fusion.7
  209.2 1.6 fusion.4
  210.8 0.6 constant_dynamic-slice_fusion.2
  211.4 0.6 constant_dynamic-slice_fusion.1
  212.0 0.6 constant_dynamic-slice_fusion
  212.6 0.7 copy.18
  213.3 0.6 copy.19
  (10 shorter events, 0.0 us)
Async XLA Ops:
  0.6 4.9 %copy-start.5 = (s32[96]{0:T(128)S(1)}, s32[96]{0:T(128)}, u32[]{:S(2)}) copy-start(s32[96]{0:T(128)} %param.11) | copy-start | bytes 1156
  148.6 8.9 %copy-start.1 = (bf16[256,1024]{1,0:T(8,128)(2,1)S(1)}, bf16[256,1024]{1,0:T(8,128)(2,1)}, u32[]{:S(2)}) copy-start(bf16[256,1024]{1,0:T(8,128)(2,1)} %get-tuple-element.24) | copy-start | bytes 1572868
  148.6 8.9 %copy-start.2 = (bf16[256,1024]{1,0:T(8,128)(2,1)S(1)}, bf16[256,1024]{1,0:T(8,128)(2,1)}, u32[]{:S(2)}) copy-start(bf16[256,1024]{1,0:T(8,128)(2,1)} %get-tuple-element.25) | copy-start | bytes 1572868
  148.6 9.2 %copy-start = (bf16[256,4096]{1,0:T(8,128)(2,1)S(1)}, bf16[256,4096]{1,0:T(8,128)(2,1)}, u32[]{:S(2)}) copy-start(bf16[256,4096]{1,0:T(8,128)(2,1)} %get-tuple-element.23) | copy-start | bytes 6291460
  208.5 4.1 %copy-start.3 = (bf16[96,2048]{1,0:T(8,128)(2,1)S(1)}, bf16[96,2048]{1,0:T(8,128)(2,1)}, u32[]{:S(2)}) copy-start(bf16[96,2048]{1,0:T(8,128)(2,1)} %get-tuple-element.51) | copy-start | bytes 1179652
  208.5 4.8 %copy-start.4 = (f32[1,2048]{1,0:T(1,128)S(1)}, f32[1,2048]{1,0:T(1,128)}, u32[]{:S(2)}) copy-start(f32[1,2048]{1,0:T(1,128)} %get-tuple-element.27) | copy-start | bytes 24580
where the time goes:
time: 214 us
  Pallas kernels  188 us (88%)
  other arithmetic  18 us (8%)
  local copies, waits for them, and re-layouts  7.41 us (3%)
    pallas_call x1, Pallas kernels, front(): pl.pallas_call(functools.partial(front_kernel, chunks, line, tp_count, sh...  142 us
    pallas_call x1, Pallas kernels, back(): pl.pallas_call(functools.partial(back_kernel, line, tp_count, kv_here), o...  46.1 us
    reduce_max x3, other arithmetic, on_device(): jnp.max(jnp.abs(block), axis=1)  4.5 us
    div x2, other arithmetic, on_device(): smooth_part[:, None] * block.astype(jnp.float32) / column_scale[None, :]  4.31 us

commit v1 on v0

v1 whole, which is shorter than its diff:
```python
import functools
import math

import jax
import jax.numpy as jnp
from jax import lax
from jax.experimental import pallas as pl
from jax.experimental.pallas import tpu as pltpu
from jax.sharding import PartitionSpec as P

HEAD = 128
KVH = 8
QHEADS = 32
GROUP = QHEADS // KVH
LANES = 128
FAR = 1 << 30

MESH = pl.DeviceIdType.MESH
QUAD = 4


def column_chunks(widths, most=GROUP * HEAD):
    return [
        (which, start, min(most, widths[which] - start))
        for which in (1, 2, 0)
        for start in range(0, widths[which], most)
    ]


def as_column(row):
    return jnp.transpose(jnp.broadcast_to(row, (LANES, LANES)))

def main_kernel(
    chunks,
    line,
    tp_count,
    share,
    hidden_ref,
    gain_ref,
    doc_ref,
    inverse_ref,
    wq_ref,
    wk_ref,
    wv_ref,
    out_ref,
    out_peak_ref,
    scale_ref,
    folded_ref,
    smooth_ref,
    relaid_ref,
    normed,
    root,
    cosine,
    sine,
    doc_row,
    docs,
    bias,
    tokens,
    mine,
    theirs,
    held_q,
    held_k,
    held_v,
    partial,
    from_left,
    from_right,
    query,
    cache,
    relaid,
    channel,
    column,
    column_tp,
    column_line,
    out_mine,
    out_all,
    w_send,
    w_recv,
    t_send,
    t_recv,
    m_send,
    m_recv,
    x_send,
    x_recv,
    x_local,
    r_send,
    r_recv,
    l_send,
    l_recv,
    p_send,
    p_recv,
    d_send,
    d_recv,
    z_send,
    z_recv,
    y_send,
    y_recv,
    s_send,
    s_recv,
    c_send,
    c_recv,
    b_send,
    b_recv,
    a_send,
    a_recv,
    o_send,
    o_recv,
):
    me = lax.axis_index("tok")
    tp = lax.axis_index("tp")
    tok_count = line * QUAD
    quad = lax.rem(me, QUAD)
    place = me // QUAD
    rows = wq_ref.shape[0]
    tok_dev = hidden_ref.shape[0]
    depth = hidden_ref.shape[1]
    width = QUAD * rows
    keys = tok_dev * tok_count
    sib = me + 1 - 2 * lax.rem(me, 2)
    side = me + 2 - 4 * (quad // 2)
    side_sib = side + 1 - 2 * lax.rem(me, 2)
    own = (wq_ref, wk_ref, wv_ref)
    held = (held_q, held_k, held_v)
    widths = [ref.shape[1] for ref in own]
    sub = rows // tp_count
    count = len(chunks)
    kv_chunks = [c for c in range(count) if chunks[c][0] > 0]
    q_chunks = [c for c in range(count) if chunks[c][0] == 0]
    kv_here = widths[1] // HEAD

    def remote(src, dst, send, recv, tok, tp_to=None):
        return pltpu.make_async_remote_copy(
            src_ref=src,
            dst_ref=dst,
            send_sem=send,
            recv_sem=recv,
            device_id=(tok, tp if tp_to is None else tp_to),
            device_id_type=MESH,
        )

    def rows_of(tok):
        return pl.ds(pl.multiple_of(tok * tok_dev, 16), tok_dev)

    def meet(barrier):
        def greet(step, carry):
            other = lax.rem(me + step, tok_count)
            pl.semaphore_signal(
                barrier, inc=1, device_id=(other, tp), device_id_type=MESH
            )
            return carry

        lax.fori_loop(1, tok_count, greet, 0)
        for step in range(1, tp_count):
            other = lax.rem(tp + step, tp_count)
            pl.semaphore_signal(
                barrier, inc=1, device_id=(me, other), device_id_type=MESH
            )

    def w_copy(kind, c):
        which, start, size = chunks[c]
        cols = pl.ds(start, size)
        if kind == 2:
            src = held[which].at[1, :, cols]
        else:
            src = own[which].at[:, cols]
        return remote(
            src,
            held[which].at[kind, :, cols],
            w_send.at[kind, c],
            w_recv.at[kind, c],
            side if kind == 1 else sib,
        )

    part = tok_dev // share
    piece = lax.rem(tp, share)
    mate = tp + 1 - 2 * piece
    first = pl.multiple_of(piece * part, 16)

    def t_copy(step):
        to = lax.rem(place + step, line)
        return remote(
            normed.at[pl.ds(first, part), pl.ds(pl.multiple_of(to * width, 128), width)],
            tokens.at[pl.ds(pl.multiple_of(place * tok_dev + first, 16), part)],
            t_send.at[step],
            t_recv.at[step],
            to * QUAD + quad,
        )

    def m_copy(step):
        source = lax.rem(place - step + line, line)
        start = pl.multiple_of(source * tok_dev + piece * part, 16)
        got = tokens.at[pl.ds(start, part)]
        return remote(got, got, m_send.at[step], m_recv.at[step], me, mate)

    wide = [sum(widths[:i]) * tp_count for i in range(3)]

    def x_copy(which, step):
        to = lax.rem(tp + step, tp_count)
        size = widths[which]
        src = own[which].at[pl.ds(pl.multiple_of(to * sub, 16), sub)]
        dst = relaid.at[:, pl.ds(pl.multiple_of(wide[which] + tp * size, 128), size)]
        if step == 0:
            return pltpu.make_async_copy(src, dst, x_local.at[which])
        return remote(src, dst, x_send.at[which, step], x_recv.at[which, step], me, to)

    relaid_out = pltpu.make_async_copy(relaid, relaid_ref, x_local.at[3])

    def d_copy(step):
        return remote(
            doc_row,
            docs.at[me],
            d_send.at[step],
            d_recv.at[step],
            lax.rem(me + step, tok_count),
        )

    def p_copy(kind):
        return remote(
            mine,
            theirs.at[kind],
            p_send.at[kind],
            p_recv.at[kind],
            (sib, side, side_sib)[kind],
        )

    def each(copy, act):
        def go(step, carry):
            getattr(copy(step), act)()
            return carry

        lax.fori_loop(1, tok_count, go, 0)

    def normalise(start, size, base):
        def go(i, carry):
            for j in range(4):
                cols = pl.ds(pl.multiple_of(base + (4 * i + j) * LANES, LANES), LANES)
                block = hidden_ref[pl.ds(start, size), cols].astype(jnp.float32)
                block = block * root[pl.ds(start, size), :] * gain_ref[:, cols]
                normed[pl.ds(start, size), cols] = block.astype(jnp.bfloat16)
            return carry

        lax.fori_loop(0, width // (4 * LANES), go, 0)

    barrier = pltpu.get_barrier_semaphore()
    meet(barrier)
    doc_row[...] = jnp.full(doc_row.shape, FAR, jnp.int32)
    doc_row[:, :tok_dev] = doc_ref[...]
    docs[me] = doc_row[...]

    def squares(i, total):
        for j in range(4):
            cols = pl.ds(pl.multiple_of((4 * i + j) * LANES, LANES), LANES)
            block = hidden_ref[:, cols].astype(jnp.float32)
            total = total + block * block
        return total

    total = lax.fori_loop(
        0, depth // (4 * LANES), squares, jnp.zeros((tok_dev, LANES), jnp.float32)
    )
    mean = jnp.sum(total, axis=1, keepdims=True) / depth
    root[...] = jnp.broadcast_to(lax.rsqrt(mean + 1e-05), (tok_dev, LANES))
    pl.semaphore_wait(barrier, tok_count - 1 + tp_count - 1)

    for c in range(count):
        w_copy(1, c).start()
        w_copy(0, c).start()

    def send_tokens(i, carry):
        step = jnp.where(2 * place < line, line - i, i)
        normalise(first, part, lax.rem(place + step, line) * width)
        t_copy(step).start()
        return carry

    lax.fori_loop(1, line, send_tokens, 0)
    normalise(0, tok_dev, place * width)
    tokens[rows_of(place)] = normed[:, pl.ds(pl.multiple_of(place * width, 128), width)]
    each(d_copy, "start")

    positions = me * tok_dev + lax.broadcasted_iota(jnp.int32, (tok_dev, HEAD), 0)
    angles = positions.astype(jnp.float32) * inverse_ref[...]
    lane = lax.broadcasted_iota(jnp.int32, (tok_dev, HEAD), 1)
    cosine[...] = jnp.cos(angles)
    sine[...] = jnp.where(lane < HEAD // 2, -1.0, 1.0) * jnp.sin(angles)

    near = sorted(range(1, line), key=lambda step: min(step, line - step))
    for step in near:
        t_copy(step).wait_recv()
        if share == 2:
            m_copy(step).start()
    for which in (1, 2, 0):
        for step in range(tp_count):
            x_copy(which, step).start()
    if share == 2:
        for step in near:
            m_copy(step).wait_recv()

    base_of = [sum(size for _, _, size in chunks[:c]) for c in range(count)]

    def span(c):
        return slice(base_of[c], base_of[c] + chunks[c][2])

    def block(d):
        return pl.ds(pl.multiple_of(d * tok_dev, 8), tok_dev)

    def right(c, d):
        cols = span(c)
        return remote(
            partial.at[block(d), cols],
            from_left.at[block(d), cols],
            r_send.at[c, d],
            r_recv.at[c, d],
            me + QUAD,
        )

    def left(c, d):
        cols = span(c)
        return remote(
            partial.at[block(d), cols],
            from_right.at[block(d), cols],
            l_send.at[c, d],
            l_recv.at[c, d],
            me - QUAD,
        )

    def add_left(c, d):
        right(c, d).wait_recv()
        cols = span(c)
        partial[block(d), cols] = partial[block(d), cols] + from_left[block(d), cols]

    def add_right(c, d):
        left(c, d).wait_recv()
        cols = span(c)
        partial[block(d), cols] = partial[block(d), cols] + from_right[block(d), cols]

    def first_sends(c):
        @pl.when(place == 0)
        def _():
            def go(i, carry):
                right(c, line - 1 - i).start()
                return carry

            lax.fori_loop(0, line - 1, go, 0)

        @pl.when(place == line - 1)
        def _():
            def go(i, carry):
                left(c, i).start()
                return carry

            lax.fori_loop(0, line - 1, go, 0)

    def reduce_step(c, i):
        to_right = line - 1 - i

        @pl.when((place > 0) & (to_right > place))
        def _():
            add_left(c, to_right)
            right(c, to_right).start()

        @pl.when((place < line - 1) & (i < place))
        def _():
            add_right(c, i)
            left(c, i).start()

    def reduce(c):
        def go(i, carry):
            reduce_step(c, i)
            return carry

        lax.fori_loop(0, line, go, 0)

    def finish(c):
        @pl.when(place > 0)
        def _():
            add_left(c, place)

        @pl.when(place < line - 1)
        def _():
            add_right(c, place)

        which, start, size = chunks[c]
        for head in range(size // HEAD):
            base = base_of[c] + head * HEAD
            states = partial[block(place), base : base + HEAD]
            if which < 2:
                states = (
                    states * cosine[...]
                    + pltpu.roll(states, HEAD // 2, 1) * sine[...]
                )
            at = start + head * HEAD + (widths[1] if which == 2 else 0)
            if which == 0:
                query[:, at : at + HEAD] = states.astype(jnp.bfloat16)
            else:
                cache[rows_of(me), at : at + HEAD] = states.astype(jnp.bfloat16)

    def columns_of(tok):
        return pl.ds(pl.multiple_of(lax.rem(tok, QUAD) * rows, 128), rows)

    def project(c):
        which, start, size = chunks[c]
        cols = slice(start, start + size)
        w_copy(1, c).wait_recv()
        w_copy(2, c).start()
        total = jnp.dot(
            tokens[:, columns_of(me)],
            own[which][:, cols],
            preferred_element_type=jnp.float32,
        )
        total += jnp.dot(
            tokens[:, columns_of(side)],
            held[which][1, :, cols],
            preferred_element_type=jnp.float32,
        )
        w_copy(0, c).wait_recv()
        total += jnp.dot(
            tokens[:, columns_of(sib)],
            held[which][0, :, cols],
            preferred_element_type=jnp.float32,
        )
        w_copy(2, c).wait_recv()
        total += jnp.dot(
            tokens[:, columns_of(side_sib)],
            held[which][2, :, cols],
            preferred_element_type=jnp.float32,
        )
        partial[:, span(c)] = total
        first_sends(c)

    def kv_rows(spot, of_side=False):
        at = lax.rem(side, QUAD) if of_side else quad
        return cache.at[rows_of(spot * QUAD + at)]

    def z_copy(way, step):
        spot = place - step if way == 0 else place + step
        to = me + QUAD if way == 0 else me - QUAD
        got = kv_rows(spot)
        return remote(got, got, z_send.at[way, step], z_recv.at[way, step], to)

    def y_copy(spot):
        got = kv_rows(spot)
        return remote(got, got, y_send.at[spot], y_recv.at[spot], side)

    def y_arrival(spot):
        got = kv_rows(spot, True)
        return remote(got, got, y_send.at[spot], y_recv.at[spot], side)

    def s_copy(spot, of_side):
        got = kv_rows(spot, of_side)
        slot = spot + (line if of_side else 0)
        return remote(got, got, s_send.at[slot], s_recv.at[slot], sib)

    def s_arrival(spot, of_side):
        at = lax.rem(side_sib if of_side else sib, QUAD)
        got = cache.at[rows_of(spot * QUAD + at)]
        slot = spot + (line if of_side else 0)
        return remote(got, got, s_send.at[slot], s_recv.at[slot], sib)

    def has(way, step):
        return place >= step if way == 0 else place + step < line

    def onward(way):
        return place + 1 < line if way == 0 else place > 0

    def kv_start():
        for way in range(2):

            @pl.when(onward(way))
            def _():
                z_copy(way, 0).start()

        y_copy(place).start()
        s_copy(place, False).start()

    def z_arrival(way, step):
        spot = place - step if way == 0 else place + step
        to = me + QUAD if way == 0 else me - QUAD
        got = kv_rows(spot)
        return remote(got, got, z_send.at[way, step - 1], z_recv.at[way, step - 1], to)

    def kv_step(step):
        for way in range(2):

            @pl.when(has(way, step))
            def _():
                z_arrival(way, step).wait_recv()

                @pl.when(onward(way))
                def _():
                    z_copy(way, step).start()

                spot = place - step if way == 0 else place + step
                y_copy(spot).start()
                s_copy(spot, False).start()

    def kv_side():
        def go(spot, carry):
            y_arrival(spot).wait_recv()
            s_copy(spot, True).start()
            return carry

        lax.fori_loop(0, line, go, 0)

    def kv_ready():
        def go(spot, carry):
            s_arrival(spot, False).wait_recv()
            s_arrival(spot, True).wait_recv()
            return carry

        lax.fori_loop(0, line, go, 0)

    def mask():
        each(d_copy, "wait")
        wanted = jnp.transpose(
            jnp.broadcast_to(doc_row[...].astype(jnp.float32), (LANES, LANES))
        )[:tok_dev]

        def go(tok, total):
            before = docs[tok].astype(jnp.float32) < wanted
            return total + jnp.where(before, 1.0, 0.0)

        total = lax.fori_loop(
            0, tok_count, go, jnp.zeros((tok_dev, LANES), jnp.float32)
        )
        since = jnp.sum(total, axis=1, keepdims=True).astype(jnp.int32)
        spot = lax.broadcasted_iota(jnp.int32, (tok_dev, keys), 0) + me * tok_dev
        at = lax.broadcasted_iota(jnp.int32, (tok_dev, keys), 1)
        bias[...] = jnp.where((at >= since) & (at <= spot), 0.0, -1e30)

    turn = math.log2(math.e) / math.sqrt(HEAD)

    def attend(g):
        heads = [
            slice((g * GROUP + h) * HEAD, (g * GROUP + h + 1) * HEAD)
            for h in range(GROUP)
        ]
        asked = jnp.concatenate([query[:, head] for head in heads], axis=0)
        key = cache[:, g * HEAD : (g + 1) * HEAD]
        value = cache[:, (kv_here + g) * HEAD : (kv_here + g + 1) * HEAD]
        scores = lax.dot_general(
            asked, key, (((1,), (1,)), ((), ())), preferred_element_type=jnp.float32
        )
        scores = (
            scores.reshape(GROUP, tok_dev, keys) + bias[...][None]
        ).reshape(GROUP * tok_dev, keys)
        weights = jnp.exp2((scores - jnp.max(scores, axis=1, keepdims=True)) * turn)
        totals = jnp.sum(weights, axis=1, keepdims=True)
        mixed = jnp.dot(
            weights.astype(jnp.bfloat16), value, preferred_element_type=jnp.float32
        )
        mixed = (mixed / totals).astype(jnp.bfloat16)
        for h, head in enumerate(heads):
            piece = mixed[h * tok_dev : (h + 1) * tok_dev]
            out_ref[:, head] = piece
            out_mine[:, head] = jnp.max(
                jnp.abs(piece.astype(jnp.float32)), axis=0, keepdims=True
            )
        cols = pl.ds(g * GROUP * HEAD, GROUP * HEAD)
        out_all[me, :, cols] = out_mine[:, cols]
        each(functools.partial(o_copy, g), "start")

    def o_copy(g, step):
        cols = pl.ds(g * GROUP * HEAD, GROUP * HEAD)
        return remote(
            out_mine.at[:, cols],
            out_all.at[me, :, cols],
            o_send.at[g, step],
            o_recv.at[g, step],
            lax.rem(me + step, tok_count),
        )

    def smooth():
        for kind in range(3):
            p_copy(kind).wait()
        peak = jnp.maximum(
            jnp.maximum(mine[...], theirs[0]), jnp.maximum(theirs[1], theirs[2])
        )
        mine[...] = peak
        for i in range(rows // LANES):
            here = slice(i * LANES, (i + 1) * LANES)
            at = pl.ds(pl.multiple_of(quad * rows + i * LANES, LANES), LANES)
            channel[0, here] = as_column(mine[:, at])
            at = pl.ds(pl.multiple_of(me * rows + i * LANES, LANES), LANES)
            channel[1, here] = as_column(gain_ref[:, at])
        for which in range(3):
            for step in range(tp_count):
                if step == 0:
                    x_copy(which, 0).wait()
                else:
                    x_copy(which, step).wait_send()
                    x_copy(which, step).wait_recv()
        relaid_out.start()
        tiles = relaid.shape[1] // LANES

        def tallest(i, most):
            cols = pl.ds(pl.multiple_of(i * LANES, LANES), LANES)
            return jnp.maximum(most, jnp.abs(relaid[:, cols].astype(jnp.float32)))

        most = lax.fori_loop(0, tiles, tallest, jnp.zeros((sub, LANES), jnp.float32))
        weight_peak = jnp.max(most, axis=1, keepdims=True)
        ours = pl.ds(pl.multiple_of(tp * sub, 16), sub)
        factor = jnp.sqrt(jnp.maximum(channel[0, ours, :], 1e-05)) / jnp.sqrt(
            jnp.maximum(weight_peak, 1e-05)
        )
        smooth_ref[...] = factor
        channel[0, ours, :] = channel[1, ours, :] / factor

        def highest(i, carry):
            cols = pl.ds(pl.multiple_of(i * LANES, LANES), LANES)
            column[0, :, cols] = jnp.max(
                jnp.abs(smooth_ref[...] * relaid[:, cols].astype(jnp.float32)),
                axis=0,
                keepdims=True,
            )
            return carry

        lax.fori_loop(0, tiles, highest, 0)
        for i in range(-(-sub // LANES)):
            size = min(LANES, sub - i * LANES)
            start = pl.multiple_of(tp * sub + i * LANES, 16)
            tile = channel[0, pl.ds(start, size), :]
            if size < LANES:
                tile = jnp.concatenate(
                    [tile, jnp.zeros((LANES - size, LANES), jnp.float32)], axis=0
                )
            folded_ref[:, i * LANES : i * LANES + size] = jnp.transpose(tile)[
                0:1, :size
            ]
        for step in range(1, tp_count):
            c_copy(step).start()

    def c_copy(step):
        return remote(
            column.at[0],
            column_tp.at[step],
            c_send.at[step],
            c_recv.at[step],
            me,
            lax.rem(tp + step, tp_count),
        )

    def b_copy(stage):
        return remote(
            column.at[1 + stage],
            column_tp.at[tp_count + stage],
            b_send.at[stage],
            b_recv.at[stage],
            (sib, side)[stage],
        )

    def a_copy(step):
        return remote(
            column.at[3],
            column_line.at[step],
            a_send.at[step],
            a_recv.at[step],
            lax.rem(place + step, line) * QUAD + quad,
        )

    def columns_tp():
        joined = column[0]
        for step in range(1, tp_count):
            c_copy(step).wait()
            joined = jnp.maximum(joined, column_tp[step])
        column[1] = joined
        b_copy(0).start()

    def columns_sib():
        b_copy(0).wait()
        column[2] = jnp.maximum(column[1], column_tp[tp_count])
        b_copy(1).start()

    def columns_side():
        b_copy(1).wait()
        column[3] = jnp.maximum(column[2], column_tp[tp_count + 1])
        for step in range(1, line):
            a_copy(step).start()

    def columns_line():
        joined = column[3]
        for step in range(1, line):
            a_copy(step).wait()
            joined = jnp.maximum(joined, column_line[step])
        scale_ref[...] = jnp.maximum(joined, 1e-05) / 127.0

    last = count - 1
    lead = len(kv_chunks)
    after = {}
    todo = []

    def plan(c, task):
        if c < last:
            after.setdefault(c, []).append(task)
        else:
            todo.append(task)

    def early():
        mine[...] = jnp.max(
            jnp.abs(tokens[...].astype(jnp.float32)), axis=0, keepdims=True
        )
        for kind in range(3):
            p_copy(kind).start()

    for c in kv_chunks:
        plan(lead, functools.partial(finish, c))
    plan(lead, kv_start)
    plan(lead, mask)
    plan(lead + 1, functools.partial(kv_step, 1))
    plan(lead + 1, smooth)
    plan(lead + 2, columns_tp)
    for step in range(2, line):
        plan(lead + 2, functools.partial(kv_step, step))
    for c in range(count):
        project(c)
        if c == 0:
            early()
        if c > 0 and c < last:
            reduce(c - 1)
        if c - 2 >= lead:
            finish(c - 2)
        for task in after.get(c, ()):
            task()
    if lead + 2 < last:
        columns_sib()
    reduce(last - 1)
    for task in todo:
        task()
    kv_side()
    if lead + 2 >= last:
        columns_sib()
    kv_ready()
    columns_side()
    waiting = [c for c in range(lead, count)]
    steps = list(range(line))
    for c in waiting:
        if c == last:
            while steps:
                reduce_step(last, steps.pop(0))
        if c >= last - 1:
            finish(c)
        attend(c - lead)
        if steps and c < last:
            reduce_step(last, steps.pop(0))
    columns_line()
    for g in range(len(q_chunks)):
        each(functools.partial(o_copy, g), "wait")
    out_peak_ref[...] = jnp.max(out_all[...], axis=0)

    for step in range(1, line):
        t_copy(step).wait_send()
        if share == 2:
            m_copy(step).wait_send()
    for c in range(count):
        for kind in range(3):
            w_copy(kind, c).wait_send()

        def sent(d, carry):
            @pl.when(d > place)
            def _():
                right(c, d).wait_send()

            @pl.when(d < place)
            def _():
                left(c, d).wait_send()

            return carry

        lax.fori_loop(0, line, sent, 0)

    def kv_sent(spot, carry):
        y_copy(spot).wait_send()
        s_copy(spot, False).wait_send()
        s_copy(spot, True).wait_send()
        return carry

    lax.fori_loop(0, line, kv_sent, 0)
    for way in range(2):
        for step in range(line - 1):

            @pl.when(has(way, step) & onward(way))
            def _():
                z_copy(way, step).wait_send()

    relaid_out.wait()


def calibrate(hidden, gain, doc_row, inverse, matrices):
    tok_count, tp_count = lax.axis_size("tok"), lax.axis_size("tp")
    line = tok_count // QUAD
    tok_dev, depth = hidden.shape
    rows = matrices[0].shape[0]
    sub = rows // tp_count
    widths = [matrix.shape[1] for matrix in matrices]
    chunks = column_chunks(widths)
    count = len(chunks)
    total = sum(widths)
    share = 2 if tp_count % 2 == 0 and tok_dev % 32 == 0 else 1
    vmem = pl.BlockSpec(memory_space=pltpu.VMEM)
    dma = pltpu.SemaphoreType.DMA
    f32, bf16 = jnp.float32, jnp.bfloat16
    queries = widths[0] // (GROUP * HEAD)
    lanes = tok_dev + -tok_dev % LANES
    return pl.pallas_call(
        functools.partial(main_kernel, chunks, line, tp_count, share),
        out_shape=(
            jax.ShapeDtypeStruct((tok_dev, widths[0]), bf16),
            jax.ShapeDtypeStruct((1, widths[0]), f32),
            jax.ShapeDtypeStruct((1, total * tp_count), f32),
            jax.ShapeDtypeStruct((1, sub), f32),
            jax.ShapeDtypeStruct((sub, LANES), f32),
            jax.ShapeDtypeStruct((sub, total * tp_count), bf16),
        ),
        in_specs=[vmem] * 7,
        out_specs=(vmem,) * 5 + (pl.BlockSpec(memory_space=pl.ANY),),
        scratch_shapes=[
            pltpu.VMEM((tok_dev, depth), bf16),
            pltpu.VMEM((tok_dev, LANES), f32),
            pltpu.VMEM((tok_dev, HEAD), f32),
            pltpu.VMEM((tok_dev, HEAD), f32),
            pltpu.VMEM((1, lanes), jnp.int32),
            pltpu.VMEM((tok_count, 1, lanes), jnp.int32),
            pltpu.VMEM((tok_dev, tok_dev * tok_count), f32),
            pltpu.VMEM((line * tok_dev, QUAD * rows), bf16),
            pltpu.VMEM((1, QUAD * rows), f32),
            pltpu.VMEM((3, 1, QUAD * rows), f32),
        ]
        + [pltpu.VMEM((3, rows, width), bf16) for width in widths]
        + [pltpu.VMEM((line * tok_dev, total), f32)] * 3
        + [
            pltpu.VMEM((tok_dev, widths[0]), bf16),
            pltpu.VMEM((tok_dev * tok_count, widths[1] + widths[2]), bf16),
            pltpu.VMEM((sub, total * tp_count), bf16),
            pltpu.VMEM((2, rows, LANES), f32),
            pltpu.VMEM((4, 1, total * tp_count), f32),
            pltpu.VMEM((tp_count + 2, 1, total * tp_count), f32),
            pltpu.VMEM((line, 1, total * tp_count), f32),
            pltpu.VMEM((1, widths[0]), f32),
            pltpu.VMEM((tok_count, 1, widths[0]), f32),
        ]
        + [dma((3, count))] * 2
        + [dma((line,))] * 4
        + [dma((3, tp_count))] * 2
        + [dma((4,))]
        + [dma((count, line))] * 4
        + [dma((3,))] * 2
        + [dma((tok_count,))] * 2
        + [dma((2, line))] * 2
        + [dma((line,))] * 2
        + [dma((2 * line,))] * 2
        + [dma((tp_count,))] * 2
        + [dma((2,))] * 2
        + [dma((line,))] * 2
        + [dma((queries, tok_count))] * 2,
        compiler_params=pltpu.CompilerParams(
            collective_id=0, has_side_effects=True, vmem_limit_bytes=63 * 1024 * 1024
        ),
    )(hidden, gain, doc_row, inverse, *matrices)


def on_device(hidden, norm_gain, w_query, w_key, w_value, doc_ids):
    tp_count = lax.axis_size("tp")
    tp_index = lax.axis_index("tp")
    matrices = (w_query, w_key, w_value)
    half = HEAD // 2
    inverse = jnp.exp(
        jnp.arange(half, dtype=jnp.float32) * (-2.0 * math.log(10000.0) / HEAD)
    )
    inverse = jnp.concatenate([inverse, inverse])[None]
    attended, out_scale, every, folded, smooth, relaid = calibrate(
        hidden, norm_gain[None], doc_ids[None], inverse, matrices
    )
    out_scale = out_scale[0]
    every = every[0]
    ends = [matrix.shape[1] * tp_count for matrix in matrices]
    bounds = [ends[0], ends[0] + ends[1]]
    every_scale = jnp.split(every, bounds)
    blocks = jnp.split(relaid, bounds, axis=1)
    scales = tuple(
        lax.dynamic_slice_in_dim(scale, tp_index * matrix.shape[1], matrix.shape[1])
        for scale, matrix in zip(every_scale, matrices)
    )
    codes = tuple(
        smooth[:, :1] * block.astype(jnp.float32) / column_scale[None, :]
        for block, column_scale in zip(blocks, every_scale)
    )
    return (attended, out_scale, folded[0], *codes, *scales)


def solution(mesh):
    in_specs = (P("tok", None), P(), P("tok", "tp"), P("tok", "tp"), P("tok", "tp"), P("tok"))
    out_specs = (
        P("tok", "tp"),
        P("tp"),
        P(("tok", "tp")),
        P(("tok", "tp"), None),
        P(("tok", "tp"), None),
        P(("tok", "tp"), None),
        P("tp"),
        P("tp"),
        P("tp"),
    )
    return jax.shard_map(
        on_device, mesh=mesh, in_specs=in_specs, out_specs=out_specs, check_vma=False
    )
```

time: 214 us -> 182 us (0.85)
  Pallas kernels: 188 us -> 166 us
  other arithmetic: 18 us -> 6.85 us
    pallas_call x2 -> x1, Pallas kernels: 188 us -> 166 us  [calibrate(): pl.pallas_call(functools.partial(main_kernel, chunks, line, tp_count, sha...]
    reduce_max x5 -> x0, other arithmetic: 5.28 us -> none  [the longest x3 4.5 us: on_device(): jnp.max(jnp.abs(block), axis=1)]
    convert_element_type x2 -> x0, other arithmetic: 3.02 us -> none  [the longest x1 3.02 us: on_device(): normed = (states * lax.rsqrt(jnp.mean(states * states, axis=1, keepdims=T...]
    unnamed x14 -> x9, local copies, waits for them, and re-layouts: 1.37 us -> 3.83 us
    div x3 -> x2, other arithmetic: 5.63 us -> 6.25 us  [on_device(): smooth[:, :1] * block.astype(jnp.float32) / column_scale[None, :]]
where the time goes in v1:
time: 182 us
  Pallas kernels  166 us (91%)
  local copies, waits for them, and re-layouts  7.68 us (4%)
  other arithmetic  6.85 us (4%)
    pallas_call x1, Pallas kernels, calibrate(): pl.pallas_call(functools.partial(main_kernel, chunks, line, tp_count, sha...  166 us
    div x2, other arithmetic, on_device(): smooth[:, :1] * block.astype(jnp.float32) / column_scale[None, :]  6.25 us
    unnamed x9, local copies, waits for them, and re-layouts  3.83 us

profile of v1, /device:TPU:0, one launch (start us, length us, event | category | flops | bytes accessed | tf_op | source)
XLA Modules:
  0.0 181.7 jit_solution(9064848366687228016)
XLA Ops:
  0.7 0.6 maximum_bitcast_fusion.inverse_ref
  1.2 166.5 %shard_map.133 = (bf16[96,2048]{1,0:T(8,128)(2,1)}, f32[1,2048]{1,0:T(1,128)}, f32[1,6144]{1,0:T(1,128)}, f32[1,256]{1,0:T(1,128)}, f32[256,128]{1,0:T(8,128)}, /*index=5*/bf16[256,6144]{1,0:T(8,128)(2,1)}) custom-call(bf16[96,8192]{1,0:T(8,128)(2,1)} %hidden_ref.1, f32[1,8192]{1,0:T(1,128)} %bitcast.13, s32[1,96]{1,0:T(1,128)} %bitcast.21, ...), custom_call_target="tpu_custom_call" | custom-call | tf_op jit(solution)/shard_map/pallas_call | solution.py:801
  167.7 0.0 copy-start
  167.7 0.8 fusion
  168.6 1.1 slice_reduce_fusion
  169.7 0.0 copy-start.2
  169.7 0.6 copy-done.2
  170.3 0.0 copy-start.1
  170.3 2.8 %multiply_divide_fusion.1 = (f32[256,1024]{1,0:T(8,128)}, f32[256,1024]{1,0:T(8,128)}) fusion(f32[1024]{0:T(1024)S(1)} %bitcast.14, bf16[256,6144]{1,0:T(8,128)(2,1)} %get-tuple-element.19, f32[256]{0:T(256)S(1)} %slice_reduce_fusion, f32[1024]{0:T(1024)S(1)} %bitcast.15), kind=kLoop, calls=%fused_computation.1 | loop fusion | flops 1572864 | bytes 3154944 | tf_op jit(solution)/shard_map/div | solution.py:881
  173.1 0.6 constant_dynamic-slice_fusion
  173.7 0.7 split.19
  174.4 0.0 copy-done
  174.4 3.4 %multiply_divide_fusion = f32[256,4096]{1,0:T(8,128)} fusion(f32[4096]{0:T(1024)S(1)} %bitcast.12, bf16[256,6144]{1,0:T(8,128)(2,1)S(1)} %copy-done, f32[256]{0:T(256)} %copy-done.2), kind=kLoop, calls=%fused_computation | loop fusion | flops 3145728 | bytes 6308864 | tf_op jit(solution)/shard_map/div | solution.py:881
  177.8 0.6 constant_dynamic-slice_fusion.2
  178.4 0.0 copy-done.1
  178.4 0.7 copy.18
  179.2 1.3 copy.19
  180.5 1.2 copy.20
  (1 shorter events, 0.0 us)
Async XLA Ops:
  167.7 6.7 %copy-start = (bf16[256,6144]{1,0:T(8,128)(2,1)S(1)}, bf16[256,6144]{1,0:T(8,128)(2,1)}, u32[]{:S(2)}) copy-start(bf16[256,6144]{1,0:T(8,128)(2,1)} %get-tuple-element.19) | copy-start | bytes 9437188
  169.7 0.6 copy-start.2
  170.3 8.2 %copy-start.1 = (bf16[96,2048]{1,0:T(8,128)(2,1)S(1)}, bf16[96,2048]{1,0:T(8,128)(2,1)}, u32[]{:S(2)}) copy-start(bf16[96,2048]{1,0:T(8,128)(2,1)} %get-tuple-element.36) | copy-start | bytes 1179652

commit v2 on v1

--- a/solution.py
+++ b/solution.py
@@ -38,7 +38,6 @@
     hidden_ref,
     gain_ref,
     doc_ref,
-    inverse_ref,
     wq_ref,
     wk_ref,
     wv_ref,
@@ -170,26 +169,39 @@
             side if kind == 1 else sib,
         )
 
+    def weights_start(c):
+        w_copy(1, c).start()
+        w_copy(0, c).start()
+
     part = tok_dev // share
     piece = lax.rem(tp, share)
     mate = tp + 1 - 2 * piece
     first = pl.multiple_of(piece * part, 16)
 
-    def t_copy(step):
+    def columns_of(tok):
+        return pl.ds(pl.multiple_of(lax.rem(tok, QUAD) * rows, 128), rows)
+
+    members = (me, side, sib, side_sib)
+
+    def t_copy(step, k):
         to = lax.rem(place + step, line)
+        base = to * width + lax.rem(members[k], QUAD) * rows
         return remote(
-            normed.at[pl.ds(first, part), pl.ds(pl.multiple_of(to * width, 128), width)],
-            tokens.at[pl.ds(pl.multiple_of(place * tok_dev + first, 16), part)],
-            t_send.at[step],
-            t_recv.at[step],
+            normed.at[pl.ds(first, part), pl.ds(pl.multiple_of(base, 128), rows)],
+            tokens.at[
+                pl.ds(pl.multiple_of(place * tok_dev + first, 16), part),
+                columns_of(members[k]),
+            ],
+            t_send.at[step, k],
+            t_recv.at[step, k],
             to * QUAD + quad,
         )
 
-    def m_copy(step):
+    def m_copy(step, k):
         source = lax.rem(place - step + line, line)
         start = pl.multiple_of(source * tok_dev + piece * part, 16)
-        got = tokens.at[pl.ds(start, part)]
-        return remote(got, got, m_send.at[step], m_recv.at[step], me, mate)
+        got = tokens.at[pl.ds(start, part), columns_of(members[k])]
+        return remote(got, got, m_send.at[step, k], m_recv.at[step, k], me, mate)
 
     wide = [sum(widths[:i]) * tp_count for i in range(3)]
 
@@ -229,16 +241,19 @@
 
         lax.fori_loop(1, tok_count, go, 0)
 
-    def normalise(start, size, base):
+    tiles_at = math.gcd(rows // LANES, 4)
+
+    def normalise(start, size, base, reach):
         def go(i, carry):
-            for j in range(4):
-                cols = pl.ds(pl.multiple_of(base + (4 * i + j) * LANES, LANES), LANES)
+            for j in range(tiles_at):
+                at = base + (tiles_at * i + j) * LANES
+                cols = pl.ds(pl.multiple_of(at, LANES), LANES)
                 block = hidden_ref[pl.ds(start, size), cols].astype(jnp.float32)
                 block = block * root[pl.ds(start, size), :] * gain_ref[:, cols]
                 normed[pl.ds(start, size), cols] = block.astype(jnp.bfloat16)
             return carry
 
-        lax.fori_loop(0, width // (4 * LANES), go, 0)
+        lax.fori_loop(0, reach // (tiles_at * LANES), go, 0)
 
     barrier = pltpu.get_barrier_semaphore()
     meet(barrier)
@@ -260,38 +275,42 @@
     root[...] = jnp.broadcast_to(lax.rsqrt(mean + 1e-05), (tok_dev, LANES))
     pl.semaphore_wait(barrier, tok_count - 1 + tp_count - 1)
 
-    for c in range(count):
-        w_copy(1, c).start()
-        w_copy(0, c).start()
-
-    def send_tokens(i, carry):
-        step = jnp.where(2 * place < line, line - i, i)
-        normalise(first, part, lax.rem(place + step, line) * width)
-        t_copy(step).start()
-        return carry
-
-    lax.fori_loop(1, line, send_tokens, 0)
-    normalise(0, tok_dev, place * width)
+    each(d_copy, "start")
+    for c in range(min(2, count)):
+        weights_start(c)
+
+    for k in range(QUAD):
+
+        def send_tokens(i, carry):
+            step = jnp.where(2 * place < line, line - i, i)
+            to = lax.rem(place + step, line)
+            base = to * width + lax.rem(members[k], QUAD) * rows
+            normalise(first, part, base, rows)
+            t_copy(step, k).start()
+            return carry
+
+        lax.fori_loop(1, line, send_tokens, 0)
+    normalise(0, tok_dev, place * width, width)
     tokens[rows_of(place)] = normed[:, pl.ds(pl.multiple_of(place * width, 128), width)]
-    each(d_copy, "start")
 
     positions = me * tok_dev + lax.broadcasted_iota(jnp.int32, (tok_dev, HEAD), 0)
-    angles = positions.astype(jnp.float32) * inverse_ref[...]
     lane = lax.broadcasted_iota(jnp.int32, (tok_dev, HEAD), 1)
+    turns = lax.rem(lane, HEAD // 2).astype(jnp.float32)
+    angles = positions.astype(jnp.float32) * jnp.exp(
+        turns * (-2.0 * math.log(10000.0) / HEAD)
+    )
     cosine[...] = jnp.cos(angles)
     sine[...] = jnp.where(lane < HEAD // 2, -1.0, 1.0) * jnp.sin(angles)
 
     near = sorted(range(1, line), key=lambda step: min(step, line - step))
-    for step in near:
-        t_copy(step).wait_recv()
-        if share == 2:
-            m_copy(step).start()
+    for k in range(QUAD):
+        for step in near:
+            t_copy(step, k).wait_recv()
+            if share == 2:
+                m_copy(step, k).start()
     for which in (1, 2, 0):
         for step in range(tp_count):
             x_copy(which, step).start()
-    if share == 2:
-        for step in near:
-            m_copy(step).wait_recv()
 
     base_of = [sum(size for _, _, size in chunks[:c]) for c in range(count)]
 
@@ -348,25 +367,40 @@
 
             lax.fori_loop(0, line - 1, go, 0)
 
+    def rightward(c):
+        def go(i, carry):
+            @pl.when((place > 0) & (line - 1 - i > place))
+            def _():
+                add_left(c, line - 1 - i)
+                right(c, line - 1 - i).start()
+
+            return carry
+
+        lax.fori_loop(0, line - 1, go, 0)
+
+    def leftward(c):
+        def go(i, carry):
+            @pl.when((place < line - 1) & (i < place))
+            def _():
+                add_right(c, i)
+                left(c, i).start()
+
+            return carry
+
+        lax.fori_loop(0, line - 1, go, 0)
+
     def reduce_step(c, i):
-        to_right = line - 1 - i
-
-        @pl.when((place > 0) & (to_right > place))
+        @pl.when(2 * place < line)
         def _():
-            add_left(c, to_right)
-            right(c, to_right).start()
-
-        @pl.when((place < line - 1) & (i < place))
+            (rightward, leftward)[i](c)
+
+        @pl.when(2 * place >= line)
         def _():
-            add_right(c, i)
-            left(c, i).start()
+            (leftward, rightward)[i](c)
 
     def reduce(c):
-        def go(i, carry):
-            reduce_step(c, i)
-            return carry
-
-        lax.fori_loop(0, line, go, 0)
+        reduce_step(c, 0)
+        reduce_step(c, 1)
 
     def finish(c):
         @pl.when(place > 0)
@@ -392,36 +426,33 @@
             else:
                 cache[rows_of(me), at : at + HEAD] = states.astype(jnp.bfloat16)
 
-    def columns_of(tok):
-        return pl.ds(pl.multiple_of(lax.rem(tok, QUAD) * rows, 128), rows)
+    def tokens_ready(c, k):
+        if c == 0 and share == 2:
+            for step in near:
+                m_copy(step, k).wait_recv()
 
     def project(c):
         which, start, size = chunks[c]
         cols = slice(start, start + size)
-        w_copy(1, c).wait_recv()
-        w_copy(2, c).start()
+        tokens_ready(c, 0)
         total = jnp.dot(
             tokens[:, columns_of(me)],
             own[which][:, cols],
             preferred_element_type=jnp.float32,
         )
-        total += jnp.dot(
-            tokens[:, columns_of(side)],
-            held[which][1, :, cols],
-            preferred_element_type=jnp.float32,
-        )
-        w_copy(0, c).wait_recv()
-        total += jnp.dot(
-            tokens[:, columns_of(sib)],
-            held[which][0, :, cols],
-            preferred_element_type=jnp.float32,
-        )
-        w_copy(2, c).wait_recv()
-        total += jnp.dot(
-            tokens[:, columns_of(side_sib)],
-            held[which][2, :, cols],
-            preferred_element_type=jnp.float32,
-        )
+        w_copy(1, c).wait_recv()
+        w_copy(2, c).start()
+        if c + 2 < count:
+            weights_start(c + 2)
+        for k, kind in ((1, 1), (2, 0), (3, 2)):
+            tokens_ready(c, k)
+            if kind != 1:
+                w_copy(kind, c).wait_recv()
+            total += jnp.dot(
+                tokens[:, columns_of(members[k])],
+                held[which][kind, :, cols],
+                preferred_element_type=jnp.float32,
+            )
         partial[:, span(c)] = total
         first_sends(c)
 
@@ -706,10 +737,15 @@
     plan(lead + 1, functools.partial(kv_step, 1))
     plan(lead + 1, smooth)
     plan(lead + 2, columns_tp)
+    middle = list(range(2, line - 1)) if lead + 2 < last else []
     for step in range(2, line):
-        plan(lead + 2, functools.partial(kv_step, step))
+        if step not in middle:
+            plan(last, functools.partial(kv_step, step))
     for c in range(count):
         project(c)
+        if c == lead + 2:
+            for step in middle:
+                kv_step(step)
         if c == 0:
             early()
         if c > 0 and c < last:
@@ -729,7 +765,7 @@
     kv_ready()
     columns_side()
     waiting = [c for c in range(lead, count)]
-    steps = list(range(line))
+    steps = [0, 1]
     for c in waiting:
         if c == last:
             while steps:
@@ -745,9 +781,10 @@
     out_peak_ref[...] = jnp.max(out_all[...], axis=0)
 
     for step in range(1, line):
-        t_copy(step).wait_send()
-        if share == 2:
-            m_copy(step).wait_send()
+        for k in range(QUAD):
+            t_copy(step, k).wait_send()
+            if share == 2:
+                m_copy(step, k).wait_send()
     for c in range(count):
         for kind in range(3):
             w_copy(kind, c).wait_send()
@@ -782,7 +819,7 @@
     relaid_out.wait()
 
 
-def calibrate(hidden, gain, doc_row, inverse, matrices):
+def calibrate(hidden, gain, doc_row, matrices):
     tok_count, tp_count = lax.axis_size("tok"), lax.axis_size("tp")
     line = tok_count // QUAD
     tok_dev, depth = hidden.shape
@@ -808,7 +845,7 @@
             jax.ShapeDtypeStruct((sub, LANES), f32),
             jax.ShapeDtypeStruct((sub, total * tp_count), bf16),
         ),
-        in_specs=[vmem] * 7,
+        in_specs=[vmem] * 6,
         out_specs=(vmem,) * 5 + (pl.BlockSpec(memory_space=pl.ANY),),
         scratch_shapes=[
             pltpu.VMEM((tok_dev, depth), bf16),
@@ -836,7 +873,7 @@
             pltpu.VMEM((tok_count, 1, widths[0]), f32),
         ]
         + [dma((3, count))] * 2
-        + [dma((line,))] * 4
+        + [dma((line, QUAD))] * 4
         + [dma((3, tp_count))] * 2
         + [dma((4,))]
         + [dma((count, line))] * 4
@@ -852,36 +889,97 @@
         compiler_params=pltpu.CompilerParams(
             collective_id=0, has_side_effects=True, vmem_limit_bytes=63 * 1024 * 1024
         ),
-    )(hidden, gain, doc_row, inverse, *matrices)
+    )(hidden, gain, doc_row, *matrices)
+
+
+def codes_kernel(
+    widths,
+    tp_count,
+    relaid_ref,
+    smooth_ref,
+    scale_ref,
+    attended_ref,
+    peak_ref,
+    folded_ref,
+    cq_ref,
+    ck_ref,
+    cv_ref,
+    sq_ref,
+    sk_ref,
+    sv_ref,
+    out_ref,
+    out_peak_ref,
+    out_folded_ref,
+    inverse,
+):
+    tp = lax.axis_index("tp")
+
+    @pl.when(pl.program_id(0) == 0)
+    def _():
+        out_ref[...] = attended_ref[...]
+        out_peak_ref[...] = peak_ref[...]
+        out_folded_ref[...] = folded_ref[...]
+        inverse[...] = 1.0 / scale_ref[...]
+        for which, ref in enumerate((sq_ref, sk_ref, sv_ref)):
+            base = sum(widths[:which]) * tp_count + tp * widths[which]
+            ref[...] = scale_ref[:, pl.ds(pl.multiple_of(base, 128), widths[which])]
+
+    factor = smooth_ref[...]
+    for which, ref in enumerate((cq_ref, ck_ref, cv_ref)):
+        base = sum(widths[:which]) * tp_count
+        for at in range(0, widths[which] * tp_count, LANES):
+            cols = slice(base + at, base + at + LANES)
+            ref[:, at : at + LANES] = (
+                factor * relaid_ref[:, cols].astype(jnp.float32) * inverse[:, cols]
+            )
+
+
+def coded(relaid, smooth, scale, attended, peak, folded, widths, tp_count):
+    sub, total = relaid.shape
+    block = math.gcd(sub, 128)
+    f32 = jnp.float32
+
+    def striped(width):
+        return pl.BlockSpec((block, width), lambda i: (i, 0))
+
+    def whole(array):
+        return pl.BlockSpec(array.shape, lambda i: (0, 0))
+
+    full = [jax.ShapeDtypeStruct((sub, width * tp_count), f32) for width in widths]
+    part = [jax.ShapeDtypeStruct((1, width), f32) for width in widths]
+    rest = [
+        jax.ShapeDtypeStruct(array.shape, array.dtype)
+        for array in (attended, peak, folded)
+    ]
+    return pl.pallas_call(
+        functools.partial(codes_kernel, widths, tp_count),
+        grid=(sub // block,),
+        out_shape=full + part + rest,
+        in_specs=[striped(total), striped(LANES)]
+        + [whole(array) for array in (scale, attended, peak, folded)],
+        out_specs=[striped(width * tp_count) for width in widths]
+        + [whole(array) for array in part + rest],
+        scratch_shapes=[pltpu.VMEM((1, total), f32)],
+    )(relaid, smooth, scale, attended, peak, folded)
 
 
 def on_device(hidden, norm_gain, w_query, w_key, w_value, doc_ids):
-    tp_count = lax.axis_size("tp")
-    tp_index = lax.axis_index("tp")
     matrices = (w_query, w_key, w_value)
-    half = HEAD // 2
-    inverse = jnp.exp(
-        jnp.arange(half, dtype=jnp.float32) * (-2.0 * math.log(10000.0) / HEAD)
+    attended, peak, scale, folded, smooth, relaid = calibrate(
+        hidden, norm_gain[None], doc_ids[None], matrices
     )
-    inverse = jnp.concatenate([inverse, inverse])[None]
-    attended, out_scale, every, folded, smooth, relaid = calibrate(
-        hidden, norm_gain[None], doc_ids[None], inverse, matrices
+    *rows, attended, peak, folded = coded(
+        relaid,
+        smooth,
+        scale,
+        attended,
+        peak,
+        folded,
+        [matrix.shape[1] for matrix in matrices],
+        lax.axis_size("tp"),
     )
-    out_scale = out_scale[0]
-    every = every[0]
-    ends = [matrix.shape[1] * tp_count for matrix in matrices]
-    bounds = [ends[0], ends[0] + ends[1]]
-    every_scale = jnp.split(every, bounds)
-    blocks = jnp.split(relaid, bounds, axis=1)
-    scales = tuple(
-        lax.dynamic_slice_in_dim(scale, tp_index * matrix.shape[1], matrix.shape[1])
-        for scale, matrix in zip(every_scale, matrices)
-    )
-    codes = tuple(
-        smooth[:, :1] * block.astype(jnp.float32) / column_scale[None, :]
-        for block, column_scale in zip(blocks, every_scale)
-    )
-    return (attended, out_scale, folded[0], *codes, *scales)
+    scales = [row[0] for row in rows[3:]]
+    return (attended, peak[0], folded[0], *rows[:3], *scales)
 
 
 def solution(mesh):

time: 182 us -> 135 us (0.74)
  Pallas kernels: 166 us -> 134 us
  local copies, waits for them, and re-layouts: 7.68 us -> 0 us
  other arithmetic: 6.85 us -> 0 us
    pallas_call x1, Pallas kernels: 166 us -> 129 us  [calibrate(): pl.pallas_call(functools.partial(main_kernel, chunks, line, tp_count, sha...]
    div x2 -> x0, other arithmetic: 6.25 us -> none  [on_device(): smooth[:, :1] * block.astype(jnp.float32) / column_scale[None, :]]
    pallas_call x0 -> x1, Pallas kernels: none -> 4.59 us  [coded(): pl.pallas_call(functools.partial(codes_kernel, widths, tp_count), grid=(s...]
    unnamed x9 -> x0, local copies, waits for them, and re-layouts: 3.83 us -> none
where the time goes in v2:
time: 135 us; the launch traced here: 134 us
  Pallas kernels  134 us (99%)
    pallas_call x1, Pallas kernels, calibrate(): pl.pallas_call(functools.partial(main_kernel, chunks, line, tp_count, sha...  129 us
    pallas_call x1, Pallas kernels, coded(): pl.pallas_call(functools.partial(codes_kernel, widths, tp_count), grid=(s...  4.59 us

profile of v2, /device:TPU:0, one launch (start us, length us, event | category | flops | bytes accessed | tf_op | source)
XLA Modules:
  0.0 134.5 jit_solution(14000916005307976204)
XLA Ops:
  0.6 129.2 %shard_map.133 = (bf16[96,2048]{1,0:T(8,128)(2,1)}, f32[1,2048]{1,0:T(1,128)}, f32[1,6144]{1,0:T(1,128)}, f32[1,256]{1,0:T(1,128)}, f32[256,128]{1,0:T(8,128)}, /*index=5*/bf16[256,6144]{1,0:T(8,128)(2,1)}) custom-call(bf16[96,8192]{1,0:T(8,128)(2,1)} %hidden_ref.1, f32[1,8192]{1,0:T(1,128)} %bitcast.7, s32[1,96]{1,0:T(1,128)} %bitcast.8, ...), custom_call_target="tpu_custom_call" | custom-call | tf_op jit(solution)/shard_map/pallas_call | solution.py:838
  129.8 4.6 %shard_map.134 = (f32[256,4096]{1,0:T(8,128)}, f32[256,1024]{1,0:T(8,128)}, f32[256,1024]{1,0:T(8,128)}, f32[1,2048]{1,0:T(1,128)}, f32[1,512]{1,0:T(1,128)}, /*...) custom-call(bf16[256,6144]{1,0:T(8,128)(2,1)} %get-tuple-element.24.relaid_ref, ...), custom_call_target="tpu_custom_call" | custom-call | tf_op jit(solution)/shard_map/pallas_call | solution.py:954

commit v3 on v2

--- a/solution.py
+++ b/solution.py
@@ -63,6 +63,9 @@
     partial,
     from_left,
     from_right,
+    outgoing,
+    value_left,
+    value_right,
     query,
     cache,
     relaid,
@@ -95,6 +98,8 @@
     y_recv,
     s_send,
     s_recv,
+    q_send,
+    q_recv,
     c_send,
     c_recv,
     b_send,
@@ -125,6 +130,11 @@
     kv_chunks = [c for c in range(count) if chunks[c][0] > 0]
     q_chunks = [c for c in range(count) if chunks[c][0] == 0]
     kv_here = widths[1] // HEAD
+    last = count - 1
+    lead = len(kv_chunks)
+    half = line // 2
+    base = jnp.where(2 * place < line, 0, half)
+    at_end = (place == 0) | (place == line - 1)
 
     def remote(src, dst, send, recv, tok, tp_to=None):
         return pltpu.make_async_remote_copy(
@@ -169,6 +179,8 @@
             side if kind == 1 else sib,
         )
 
+    ahead = 3
+
     def weights_start(c):
         w_copy(1, c).start()
         w_copy(0, c).start()
@@ -217,13 +229,12 @@
     relaid_out = pltpu.make_async_copy(relaid, relaid_ref, x_local.at[3])
 
     def d_copy(step):
-        return remote(
-            doc_row,
-            docs.at[me],
-            d_send.at[step],
-            d_recv.at[step],
-            lax.rem(me + step, tok_count),
-        )
+        to = lax.rem(me + step, tok_count)
+        return remote(doc_row, docs.at[me], d_send.at[0], d_recv.at[0], to)
+
+    def d_all():
+        every = docs.at[pl.ds(0, tok_count - 1)]
+        return remote(every, every, d_send.at[0], d_recv.at[0], sib)
 
     def p_copy(kind):
         return remote(
@@ -234,9 +245,9 @@
             (sib, side, side_sib)[kind],
         )
 
-    def each(copy, act):
+    def each(copy):
         def go(step, carry):
-            getattr(copy(step), act)()
+            copy(step).start()
             return carry
 
         lax.fori_loop(1, tok_count, go, 0)
@@ -275,8 +286,8 @@
     root[...] = jnp.broadcast_to(lax.rsqrt(mean + 1e-05), (tok_dev, LANES))
     pl.semaphore_wait(barrier, tok_count - 1 + tp_count - 1)
 
-    each(d_copy, "start")
-    for c in range(min(2, count)):
+    each(d_copy)
+    for c in range(min(ahead, count)):
         weights_start(c)
 
     for k in range(QUAD):
@@ -293,15 +304,19 @@
     normalise(0, tok_dev, place * width, width)
     tokens[rows_of(place)] = normed[:, pl.ds(pl.multiple_of(place * width, 128), width)]
 
-    positions = me * tok_dev + lax.broadcasted_iota(jnp.int32, (tok_dev, HEAD), 0)
     lane = lax.broadcasted_iota(jnp.int32, (tok_dev, HEAD), 1)
     turns = lax.rem(lane, HEAD // 2).astype(jnp.float32)
-    angles = positions.astype(jnp.float32) * jnp.exp(
-        turns * (-2.0 * math.log(10000.0) / HEAD)
-    )
-    cosine[...] = jnp.cos(angles)
-    sine[...] = jnp.where(lane < HEAD // 2, -1.0, 1.0) * jnp.sin(angles)
-
+    speed = jnp.exp(turns * (-2.0 * math.log(10000.0) / HEAD))
+
+    def tables(j, carry):
+        spot = ((base + j) * QUAD + quad) * tok_dev
+        spot = spot + lax.broadcasted_iota(jnp.int32, (tok_dev, HEAD), 0)
+        angles = spot.astype(jnp.float32) * speed
+        cosine[j] = jnp.cos(angles)
+        sine[j] = jnp.where(lane < HEAD // 2, -1.0, 1.0) * jnp.sin(angles)
+        return carry
+
+    lax.fori_loop(0, half, tables, 0)
     near = sorted(range(1, line), key=lambda step: min(step, line - step))
     for k in range(QUAD):
         for step in near:
@@ -320,111 +335,156 @@
     def block(d):
         return pl.ds(pl.multiple_of(d * tok_dev, 8), tok_dev)
 
+    def travels(c):
+        which, start, size = chunks[c]
+        if which == 2:
+            return outgoing, value_left, value_right, slice(start, start + size)
+        return partial, from_left, from_right, span(c)
+
     def right(c, d):
-        cols = span(c)
+        held_here, landed, _, cols = travels(c)
         return remote(
-            partial.at[block(d), cols],
-            from_left.at[block(d), cols],
+            held_here.at[block(d), cols],
+            landed.at[block(d), cols],
             r_send.at[c, d],
             r_recv.at[c, d],
             me + QUAD,
         )
 
     def left(c, d):
-        cols = span(c)
+        held_here, _, landed, cols = travels(c)
         return remote(
-            partial.at[block(d), cols],
-            from_right.at[block(d), cols],
+            held_here.at[block(d), cols],
+            landed.at[block(d), cols],
             l_send.at[c, d],
             l_recv.at[c, d],
             me - QUAD,
         )
 
-    def add_left(c, d):
-        right(c, d).wait_recv()
-        cols = span(c)
-        partial[block(d), cols] = partial[block(d), cols] + from_left[block(d), cols]
-
-    def add_right(c, d):
-        left(c, d).wait_recv()
-        cols = span(c)
-        partial[block(d), cols] = partial[block(d), cols] + from_right[block(d), cols]
+    def added(c, d, way):
+        (right, left)[way](c, d).wait_recv()
+        landed, cols = travels(c)[1 + way], travels(c)[3]
+        return partial[block(d), span(c)] + landed[block(d), cols].astype(jnp.float32)
+
+    def pass_on(c, d, way):
+        to, cols = travels(c)[0], travels(c)[3]
+        to[block(d), cols] = added(c, d, way).astype(to.dtype)
+        (right, left)[way](c, d).start()
+
+    def sends(c, way):
+        if c < last:
+            return half, (lambda i: half + i) if way == 0 else (lambda i: half - 1 - i)
+        if way == 0:
+            return line - 1, lambda i: line - 1 - i
+        return line - 1, lambda i: i
+
+    def goes(c, d, way):
+        if c < last:
+            return place < line - 1 if way == 0 else place > 0
+        return d > place if way == 0 else d < place
 
     def first_sends(c):
-        @pl.when(place == 0)
+        for way in range(2):
+
+            @pl.when(place == (0 if way == 0 else line - 1))
+            def _():
+                size, pick = sends(c, way)
+
+                def go(i, carry):
+                    (right, left)[way](c, pick(i)).start()
+                    return carry
+
+                lax.fori_loop(0, size, go, 0)
+
+    def onward(c, i, way):
+        size, pick = sends(c, way)
+        inside = place > 0 if way == 0 else place < line - 1
+        d = pick(i)
+
+        @pl.when((i < size) & inside & goes(c, d, way))
         def _():
-            def go(i, carry):
-                right(c, line - 1 - i).start()
-                return carry
-
-            lax.fori_loop(0, line - 1, go, 0)
-
-        @pl.when(place == line - 1)
-        def _():
-            def go(i, carry):
-                left(c, i).start()
-                return carry
-
-            lax.fori_loop(0, line - 1, go, 0)
-
-    def rightward(c):
-        def go(i, carry):
-            @pl.when((place > 0) & (line - 1 - i > place))
-            def _():
-                add_left(c, line - 1 - i)
-                right(c, line - 1 - i).start()
-
+            pass_on(c, d, way)
+
+    def weave(far, near):
+        def go(nearest, i):
+            if far is not None:
+                onward(far, i, 1 - nearest)
+            if near is not None:
+                onward(near, i, nearest)
+
+        def left_half(i, carry):
+            go(0, i)
             return carry
 
-        lax.fori_loop(0, line - 1, go, 0)
-
-    def leftward(c):
-        def go(i, carry):
-            @pl.when((place < line - 1) & (i < place))
-            def _():
-                add_right(c, i)
-                left(c, i).start()
-
+        def right_half(i, carry):
+            go(1, i)
             return carry
 
-        lax.fori_loop(0, line - 1, go, 0)
-
-    def reduce_step(c, i):
+        top = line - 1 if last in (far, near) else half
+
         @pl.when(2 * place < line)
         def _():
-            (rightward, leftward)[i](c)
+            lax.fori_loop(0, top, left_half, 0)
 
         @pl.when(2 * place >= line)
         def _():
-            (leftward, rightward)[i](c)
-
-    def reduce(c):
-        reduce_step(c, 0)
-        reduce_step(c, 1)
-
-    def finish(c):
-        @pl.when(place > 0)
-        def _():
-            add_left(c, place)
-
-        @pl.when(place < line - 1)
-        def _():
-            add_right(c, place)
-
+            lax.fori_loop(0, top, right_half, 0)
+
+    def settle(c, j):
         which, start, size = chunks[c]
+        d = base + j
         for head in range(size // HEAD):
-            base = base_of[c] + head * HEAD
-            states = partial[block(place), base : base + HEAD]
+            at = base_of[c] + head * HEAD
+            states = partial[block(d), at : at + HEAD]
             if which < 2:
                 states = (
-                    states * cosine[...]
-                    + pltpu.roll(states, HEAD // 2, 1) * sine[...]
+                    states * cosine[j] + pltpu.roll(states, HEAD // 2, 1) * sine[j]
                 )
             at = start + head * HEAD + (widths[1] if which == 2 else 0)
             if which == 0:
-                query[:, at : at + HEAD] = states.astype(jnp.bfloat16)
+                query[j, :, at : at + HEAD] = states.astype(jnp.bfloat16)
             else:
-                cache[rows_of(me), at : at + HEAD] = states.astype(jnp.bfloat16)
+                rows_at = rows_of(d * QUAD + quad)
+                cache[rows_at, at : at + HEAD] = states.astype(jnp.bfloat16)
+
+    def q_copy(c, j):
+        which, start, size = chunks[c]
+        got = query.at[j, :, pl.ds(start, size)]
+        to = (base + j) * QUAD + quad
+        return remote(got, got, q_send.at[c - lead, j], q_recv.at[c - lead], to)
+
+    def finish(c):
+        if c == last:
+            for way in range(2):
+
+                @pl.when(place > 0 if way == 0 else place < line - 1)
+                def _():
+                    partial[block(place), span(c)] = added(c, place, way)
+
+            settle(c, place - base)
+            return
+
+        @pl.when(at_end)
+        def _():
+            def go(i, carry):
+                j = jnp.where(place == 0, half - 1 - i, i)
+                d = base + j
+                for way in range(2):
+
+                    @pl.when(place == (line - 1 if way == 0 else 0))
+                    def _():
+                        partial[block(d), span(c)] = added(c, d, way)
+
+                settle(c, j)
+                if chunks[c][0] == 0:
+
+                    @pl.when(d != place)
+                    def _():
+                        q_copy(c, j).start()
+
+                return carry
+
+            lax.fori_loop(0, half, go, 0)
 
     def tokens_ready(c, k):
         if c == 0 and share == 2:
@@ -442,8 +502,8 @@
         )
         w_copy(1, c).wait_recv()
         w_copy(2, c).start()
-        if c + 2 < count:
-            weights_start(c + 2)
+        if c + ahead < count:
+            weights_start(c + ahead)
         for k, kind in ((1, 1), (2, 0), (3, 2)):
             tokens_ready(c, k)
             if kind != 1:
@@ -454,17 +514,18 @@
                 preferred_element_type=jnp.float32,
             )
         partial[:, span(c)] = total
+        if which == 2:
+            outgoing[:, cols] = total.astype(jnp.bfloat16)
         first_sends(c)
 
     def kv_rows(spot, of_side=False):
         at = lax.rem(side, QUAD) if of_side else quad
         return cache.at[rows_of(spot * QUAD + at)]
 
-    def z_copy(way, step):
-        spot = place - step if way == 0 else place + step
-        to = me + QUAD if way == 0 else me - QUAD
-        got = kv_rows(spot)
-        return remote(got, got, z_send.at[way, step], z_recv.at[way, step], to)
+    def z_copy(way, j):
+        got = kv_rows(j + way * half)
+        to = me - QUAD if way else me + QUAD
+        return remote(got, got, z_send.at[way, j], z_recv.at[way, j], to)
 
     def y_copy(spot):
         got = kv_rows(spot)
@@ -485,42 +546,42 @@
         slot = spot + (line if of_side else 0)
         return remote(got, got, s_send.at[slot], s_recv.at[slot], sib)
 
-    def has(way, step):
-        return place >= step if way == 0 else place + step < line
-
-    def onward(way):
-        return place + 1 < line if way == 0 else place > 0
+    def kv_pass(way, fresh):
+        def go(j, carry):
+            if not fresh:
+                z_copy(way, j).wait_recv()
+
+            @pl.when(place > 0 if way else place < line - 1)
+            def _():
+                z_copy(way, j).start()
+
+            y_copy(j + way * half).start()
+            s_copy(j + way * half, False).start()
+            return carry
+
+        lax.fori_loop(0, half, go, 0)
 
     def kv_start():
         for way in range(2):
 
-            @pl.when(onward(way))
+            @pl.when(place == way * (line - 1))
             def _():
-                z_copy(way, 0).start()
-
-        y_copy(place).start()
-        s_copy(place, False).start()
-
-    def z_arrival(way, step):
-        spot = place - step if way == 0 else place + step
-        to = me + QUAD if way == 0 else me - QUAD
-        got = kv_rows(spot)
-        return remote(got, got, z_send.at[way, step - 1], z_recv.at[way, step - 1], to)
-
-    def kv_step(step):
+                kv_pass(way, True)
+
+    def kv_near():
         for way in range(2):
-
-            @pl.when(has(way, step))
+            nearer = 2 * place >= line if way else 2 * place < line
+
+            @pl.when(nearer & jnp.logical_not(at_end))
             def _():
-                z_arrival(way, step).wait_recv()
-
-                @pl.when(onward(way))
-                def _():
-                    z_copy(way, step).start()
-
-                spot = place - step if way == 0 else place + step
-                y_copy(spot).start()
-                s_copy(spot, False).start()
+                kv_pass(way, False)
+
+    def kv_far():
+        for way in range(2):
+
+            @pl.when(2 * place < line if way else 2 * place >= line)
+            def _():
+                kv_pass(way, False)
 
     def kv_side():
         def go(spot, carry):
@@ -539,7 +600,7 @@
         lax.fori_loop(0, line, go, 0)
 
     def mask():
-        each(d_copy, "wait")
+        d_all().wait()
         wanted = jnp.transpose(
             jnp.broadcast_to(doc_row[...].astype(jnp.float32), (LANES, LANES))
         )[:tok_dev]
@@ -563,7 +624,15 @@
             slice((g * GROUP + h) * HEAD, (g * GROUP + h + 1) * HEAD)
             for h in range(GROUP)
         ]
-        asked = jnp.concatenate([query[:, head] for head in heads], axis=0)
+        if g + lead < last:
+
+            @pl.when(jnp.logical_not(at_end))
+            def _():
+                q_copy(g + lead, place - base).wait_recv()
+
+        asked = jnp.concatenate(
+            [query[place - base, :, head] for head in heads], axis=0
+        )
         key = cache[:, g * HEAD : (g + 1) * HEAD]
         value = cache[:, (kv_here + g) * HEAD : (kv_here + g + 1) * HEAD]
         scores = lax.dot_general(
@@ -586,17 +655,18 @@
             )
         cols = pl.ds(g * GROUP * HEAD, GROUP * HEAD)
         out_all[me, :, cols] = out_mine[:, cols]
-        each(functools.partial(o_copy, g), "start")
+        each(functools.partial(o_copy, g))
 
     def o_copy(g, step):
         cols = pl.ds(g * GROUP * HEAD, GROUP * HEAD)
+        to = lax.rem(me + step, tok_count)
         return remote(
-            out_mine.at[:, cols],
-            out_all.at[me, :, cols],
-            o_send.at[g, step],
-            o_recv.at[g, step],
-            lax.rem(me + step, tok_count),
-        )
+            out_mine.at[:, cols], out_all.at[me, :, cols], o_send.at[0], o_recv.at[0], to
+        )
+
+    def o_all():
+        every = out_all.at[pl.ds(0, tok_count - 1)]
+        return remote(every, every, o_send.at[0], o_recv.at[0], sib)
 
     def smooth():
         for kind in range(3):
@@ -712,17 +782,6 @@
             joined = jnp.maximum(joined, column_line[step])
         scale_ref[...] = jnp.maximum(joined, 1e-05) / 127.0
 
-    last = count - 1
-    lead = len(kv_chunks)
-    after = {}
-    todo = []
-
-    def plan(c, task):
-        if c < last:
-            after.setdefault(c, []).append(task)
-        else:
-            todo.append(task)
-
     def early():
         mine[...] = jnp.max(
             jnp.abs(tokens[...].astype(jnp.float32)), axis=0, keepdims=True
@@ -730,54 +789,68 @@
         for kind in range(3):
             p_copy(kind).start()
 
+    ran = set()
+
+    def once(act, c, *rest):
+        if c <= last and (act, c) not in ran:
+            ran.add((act, c))
+            act(c, *rest)
+
+    def pair(far, near):
+        far = None if far > last or ("far", far) in ran else far
+        near = None if near > last or ("near", near) in ran else near
+        ran.update({("far", far), ("near", near)})
+        if far is not None or near is not None:
+            weave(far, near)
+
+    def split_project(c, ends):
+        @pl.when(at_end if ends else jnp.logical_not(at_end))
+        def _():
+            project(c)
+
+    once(project, 0)
+    early()
+    for c in range(1, lead):
+        once(project, c)
+    for c in range(lead):
+        pair(c - 1 if c else FAR, c)
+    once(project, lead)
+    pair(lead - 1, lead)
     for c in kv_chunks:
-        plan(lead, functools.partial(finish, c))
-    plan(lead, kv_start)
-    plan(lead, mask)
-    plan(lead + 1, functools.partial(kv_step, 1))
-    plan(lead + 1, smooth)
-    plan(lead + 2, columns_tp)
-    middle = list(range(2, line - 1)) if lead + 2 < last else []
-    for step in range(2, line):
-        if step not in middle:
-            plan(last, functools.partial(kv_step, step))
-    for c in range(count):
-        project(c)
-        if c == lead + 2:
-            for step in middle:
-                kv_step(step)
-        if c == 0:
-            early()
-        if c > 0 and c < last:
-            reduce(c - 1)
-        if c - 2 >= lead:
-            finish(c - 2)
-        for task in after.get(c, ()):
-            task()
-    if lead + 2 < last:
-        columns_sib()
-    reduce(last - 1)
-    for task in todo:
-        task()
+        once(finish, c)
+    kv_start()
+    mask()
+    once(project, lead + 1)
+    pair(lead, FAR)
+    kv_near()
+    smooth()
+    once(project, lead + 2)
+    if lead + 3 <= last:
+        split_project(lead + 3, True)
+    kv_far()
+    pair(FAR, lead + 1)
+    if lead < last - 1:
+        once(finish, lead)
+    if lead + 3 <= last:
+        split_project(lead + 3, False)
+        ran.add((project, lead + 3))
+    pair(lead + 1, lead + 2)
+    if lead + 1 < last - 1:
+        once(finish, lead + 1)
+    columns_tp()
+    for c in range(lead, count):
+        once(project, c)
+        pair(c - 1, c)
+    columns_sib()
+    pair(last, FAR)
     kv_side()
-    if lead + 2 >= last:
-        columns_sib()
+    columns_side()
     kv_ready()
-    columns_side()
-    waiting = [c for c in range(lead, count)]
-    steps = [0, 1]
-    for c in waiting:
-        if c == last:
-            while steps:
-                reduce_step(last, steps.pop(0))
-        if c >= last - 1:
-            finish(c)
+    for c in range(lead, count):
+        once(finish, c)
         attend(c - lead)
-        if steps and c < last:
-            reduce_step(last, steps.pop(0))
     columns_line()
-    for g in range(len(q_chunks)):
-        each(functools.partial(o_copy, g), "wait")
+    o_all().wait()
     out_peak_ref[...] = jnp.max(out_all[...], axis=0)
 
     for step in range(1, line):
@@ -790,17 +863,35 @@
             w_copy(kind, c).wait_send()
 
         def sent(d, carry):
-            @pl.when(d > place)
+            if c < last:
+                to_right, to_left = d >= half, d < half
+            else:
+                to_right, to_left = d > place, d < place
+
+            @pl.when(to_right & (place < line - 1))
             def _():
                 right(c, d).wait_send()
 
-            @pl.when(d < place)
+            @pl.when(to_left & (place > 0))
             def _():
                 left(c, d).wait_send()
 
             return carry
 
         lax.fori_loop(0, line, sent, 0)
+
+    for c in range(lead, last):
+
+        @pl.when(at_end)
+        def _():
+            def q_sent(j, carry):
+                @pl.when(base + j != place)
+                def _():
+                    q_copy(c, j).wait_send()
+
+                return carry
+
+            lax.fori_loop(0, half, q_sent, 0)
 
     def kv_sent(spot, carry):
         y_copy(spot).wait_send()
@@ -810,11 +901,14 @@
 
     lax.fori_loop(0, line, kv_sent, 0)
     for way in range(2):
-        for step in range(line - 1):
-
-            @pl.when(has(way, step) & onward(way))
-            def _():
-                z_copy(way, step).wait_send()
+
+        @pl.when(place > 0 if way else place < line - 1)
+        def _():
+            def z_sent(j, carry):
+                z_copy(way, j).wait_send()
+                return carry
+
+            lax.fori_loop(0, half, z_sent, 0)
 
     relaid_out.wait()
 
@@ -850,8 +944,8 @@
         scratch_shapes=[
             pltpu.VMEM((tok_dev, depth), bf16),
             pltpu.VMEM((tok_dev, LANES), f32),
-            pltpu.VMEM((tok_dev, HEAD), f32),
-            pltpu.VMEM((tok_dev, HEAD), f32),
+            pltpu.VMEM((line // 2, tok_dev, HEAD), f32),
+            pltpu.VMEM((line // 2, tok_dev, HEAD), f32),
             pltpu.VMEM((1, lanes), jnp.int32),
             pltpu.VMEM((tok_count, 1, lanes), jnp.int32),
             pltpu.VMEM((tok_dev, tok_dev * tok_count), f32),
@@ -861,8 +955,9 @@
         ]
         + [pltpu.VMEM((3, rows, width), bf16) for width in widths]
         + [pltpu.VMEM((line * tok_dev, total), f32)] * 3
+        + [pltpu.VMEM((line * tok_dev, widths[2]), bf16)] * 3
         + [
-            pltpu.VMEM((tok_dev, widths[0]), bf16),
+            pltpu.VMEM((line // 2, tok_dev, widths[0]), bf16),
             pltpu.VMEM((tok_dev * tok_count, widths[1] + widths[2]), bf16),
             pltpu.VMEM((sub, total * tp_count), bf16),
             pltpu.VMEM((2, rows, LANES), f32),
@@ -878,14 +973,15 @@
         + [dma((4,))]
         + [dma((count, line))] * 4
         + [dma((3,))] * 2
-        + [dma((tok_count,))] * 2
-        + [dma((2, line))] * 2
+        + [dma((1,))] * 2
+        + [dma((2, line // 2))] * 2
         + [dma((line,))] * 2
         + [dma((2 * line,))] * 2
+        + [dma((queries, line // 2)), dma((queries,))]
         + [dma((tp_count,))] * 2
         + [dma((2,))] * 2
         + [dma((line,))] * 2
-        + [dma((queries, tok_count))] * 2,
+        + [dma((1,))] * 2,
         compiler_params=pltpu.CompilerParams(
             collective_id=0, has_side_effects=True, vmem_limit_bytes=63 * 1024 * 1024
         ),

time: 135 us -> 123 us (0.911)
  Pallas kernels: 134 us -> 122 us
    pallas_call x1, Pallas kernels: 129 us -> 118 us  [calibrate(): pl.pallas_call(functools.partial(main_kernel, chunks, line, tp_count, sha...]
where the time goes in v3:
time: 123 us
  Pallas kernels  122 us (99%)
    pallas_call x1, Pallas kernels, calibrate(): pl.pallas_call(functools.partial(main_kernel, chunks, line, tp_count, sha...  118 us
    pallas_call x1, Pallas kernels, coded(): pl.pallas_call(functools.partial(codes_kernel, widths, tp_count), grid=(s...  4.59 us

profile of v3, /device:TPU:0, one launch (start us, length us, event | category | flops | bytes accessed | tf_op | source)
XLA Modules:
  0.0 122.8 jit_solution(10601030112498594005)
XLA Ops:
  0.6 117.5 %shard_map.133 = (bf16[96,2048]{1,0:T(8,128)(2,1)}, f32[1,2048]{1,0:T(1,128)}, f32[1,6144]{1,0:T(1,128)}, f32[1,256]{1,0:T(1,128)}, f32[256,128]{1,0:T(8,128)}, /*index=5*/bf16[256,6144]{1,0:T(8,128)(2,1)}) custom-call(bf16[96,8192]{1,0:T(8,128)(2,1)} %hidden_ref.1, f32[1,8192]{1,0:T(1,128)} %bitcast.7, s32[1,96]{1,0:T(1,128)} %bitcast.8, ...), custom_call_target="tpu_custom_call" | custom-call | tf_op jit(solution)/shard_map/pallas_call | solution.py:932
  118.2 4.6 %shard_map.134 = (f32[256,4096]{1,0:T(8,128)}, f32[256,1024]{1,0:T(8,128)}, f32[256,1024]{1,0:T(8,128)}, f32[1,2048]{1,0:T(1,128)}, f32[1,512]{1,0:T(1,128)}, /*...) custom-call(bf16[256,6144]{1,0:T(8,128)(2,1)} %get-tuple-element.24.relaid_ref, ...), custom_call_target="tpu_custom_call" | custom-call | tf_op jit(solution)/shard_map/pallas_call | solution.py:1050

commit v4 on v3

--- a/solution.py
+++ b/solution.py
@@ -38,9 +38,9 @@
     hidden_ref,
     gain_ref,
     doc_ref,
-    wq_ref,
-    wk_ref,
-    wv_ref,
+    wq_from,
+    wk_from,
+    wv_from,
     out_ref,
     out_peak_ref,
     scale_ref,
@@ -57,15 +57,15 @@
     tokens,
     mine,
     theirs,
+    wq_ref,
+    wk_ref,
+    wv_ref,
     held_q,
     held_k,
     held_v,
     partial,
     from_left,
     from_right,
-    outgoing,
-    value_left,
-    value_right,
     query,
     cache,
     relaid,
@@ -75,6 +75,7 @@
     column_line,
     out_mine,
     out_all,
+    w_local,
     w_send,
     w_recv,
     t_send,
@@ -174,7 +175,7 @@
         return remote(
             src,
             held[which].at[kind, :, cols],
-            w_send.at[kind, c],
+            w_send.at[which],
             w_recv.at[kind, c],
             side if kind == 1 else sib,
         )
@@ -194,17 +195,24 @@
         return pl.ds(pl.multiple_of(lax.rem(tok, QUAD) * rows, 128), rows)
 
     members = (me, side, sib, side_sib)
+    cuts = 2 if rows % (2 * LANES) == 0 else 1
+    slab = rows // cuts
+
+    def channels(k):
+        start = lax.rem(members[k // cuts], QUAD) * rows + (k % cuts) * slab
+        return pl.multiple_of(start, 128)
+
 
     def t_copy(step, k):
         to = lax.rem(place + step, line)
-        base = to * width + lax.rem(members[k], QUAD) * rows
+        base = to * width + channels(k)
         return remote(
-            normed.at[pl.ds(first, part), pl.ds(pl.multiple_of(base, 128), rows)],
+            normed.at[pl.ds(first, part), pl.ds(pl.multiple_of(base, 128), slab)],
             tokens.at[
                 pl.ds(pl.multiple_of(place * tok_dev + first, 16), part),
-                columns_of(members[k]),
+                pl.ds(channels(k), slab),
             ],
-            t_send.at[step, k],
+            t_send.at[0],
             t_recv.at[step, k],
             to * QUAD + quad,
         )
@@ -212,8 +220,12 @@
     def m_copy(step, k):
         source = lax.rem(place - step + line, line)
         start = pl.multiple_of(source * tok_dev + piece * part, 16)
-        got = tokens.at[pl.ds(start, part), columns_of(members[k])]
-        return remote(got, got, m_send.at[step, k], m_recv.at[step, k], me, mate)
+        got = tokens.at[pl.ds(start, part), pl.ds(channels(k), slab)]
+        return remote(got, got, m_send.at[0], m_recv.at[step, k], me, mate)
+
+    def tokens_sent(sem):
+        every = tokens.at[pl.ds(0, (line - 1) * part)]
+        remote(every, every, sem, sem, sib).wait_send()
 
     wide = [sum(widths[:i]) * tp_count for i in range(3)]
 
@@ -223,10 +235,18 @@
         src = own[which].at[pl.ds(pl.multiple_of(to * sub, 16), sub)]
         dst = relaid.at[:, pl.ds(pl.multiple_of(wide[which] + tp * size, 128), size)]
         if step == 0:
-            return pltpu.make_async_copy(src, dst, x_local.at[which])
-        return remote(src, dst, x_send.at[which, step], x_recv.at[which, step], me, to)
-
-    relaid_out = pltpu.make_async_copy(relaid, relaid_ref, x_local.at[3])
+            return pltpu.make_async_copy(src, dst, x_local.at[0])
+        return remote(src, dst, x_send.at[0], x_recv.at[0], me, to)
+
+    def x_all():
+        size = sum(widths)
+        every = relaid.at[:, pl.ds(0, size)]
+        pltpu.make_async_copy(every, every, x_local.at[0]).wait()
+        if tp_count > 1:
+            every = relaid.at[:, pl.ds(0, (tp_count - 1) * size)]
+            remote(every, every, x_send.at[0], x_recv.at[0], sib).wait()
+
+    relaid_out = pltpu.make_async_copy(relaid, relaid_ref, x_local.at[1])
 
     def d_copy(step):
         to = lax.rem(me + step, tok_count)
@@ -240,8 +260,8 @@
         return remote(
             mine,
             theirs.at[kind],
-            p_send.at[kind],
-            p_recv.at[kind],
+            p_send.at[0],
+            p_recv.at[0],
             (sib, side, side_sib)[kind],
         )
 
@@ -252,7 +272,7 @@
 
         lax.fori_loop(1, tok_count, go, 0)
 
-    tiles_at = math.gcd(rows // LANES, 4)
+    tiles_at = math.gcd(slab // LANES, 4)
 
     def normalise(start, size, base, reach):
         def go(i, carry):
@@ -266,6 +286,12 @@
 
         lax.fori_loop(0, reach // (tiles_at * LANES), go, 0)
 
+    loads = [
+        pltpu.make_async_copy(source, own[which], w_local.at[which])
+        for which, source in enumerate((wq_from, wk_from, wv_from))
+    ]
+    for which in (1, 2, 0):
+        loads[which].start()
     barrier = pltpu.get_barrier_semaphore()
     meet(barrier)
     doc_row[...] = jnp.full(doc_row.shape, FAR, jnp.int32)
@@ -287,16 +313,17 @@
     pl.semaphore_wait(barrier, tok_count - 1 + tp_count - 1)
 
     each(d_copy)
+    for load in loads:
+        load.wait()
     for c in range(min(ahead, count)):
         weights_start(c)
 
-    for k in range(QUAD):
+    for k in range(QUAD * cuts):
 
         def send_tokens(i, carry):
             step = jnp.where(2 * place < line, line - i, i)
             to = lax.rem(place + step, line)
-            base = to * width + lax.rem(members[k], QUAD) * rows
-            normalise(first, part, base, rows)
+            normalise(first, part, to * width + channels(k), slab)
             t_copy(step, k).start()
             return carry
 
@@ -318,15 +345,11 @@
 
     lax.fori_loop(0, half, tables, 0)
     near = sorted(range(1, line), key=lambda step: min(step, line - step))
-    for k in range(QUAD):
+    for k in range(QUAD * cuts):
         for step in near:
             t_copy(step, k).wait_recv()
             if share == 2:
                 m_copy(step, k).start()
-    for which in (1, 2, 0):
-        for step in range(tp_count):
-            x_copy(which, step).start()
-
     base_of = [sum(size for _, _, size in chunks[:c]) for c in range(count)]
 
     def span(c):
@@ -335,40 +358,31 @@
     def block(d):
         return pl.ds(pl.multiple_of(d * tok_dev, 8), tok_dev)
 
-    def travels(c):
-        which, start, size = chunks[c]
-        if which == 2:
-            return outgoing, value_left, value_right, slice(start, start + size)
-        return partial, from_left, from_right, span(c)
+    def spot_of(c, d):
+        return c * half + lax.rem(d, half) if c < last else last * half + d
+
+    def sent_of(c, d):
+        return c if c < last else last + d
 
     def right(c, d):
-        held_here, landed, _, cols = travels(c)
-        return remote(
-            held_here.at[block(d), cols],
-            landed.at[block(d), cols],
-            r_send.at[c, d],
-            r_recv.at[c, d],
-            me + QUAD,
-        )
+        here = partial.at[block(d), span(c)]
+        there = from_left.at[block(d), span(c)]
+        send, recv = r_send.at[sent_of(c, d)], r_recv.at[spot_of(c, d)]
+        return remote(here, there, send, recv, me + QUAD)
 
     def left(c, d):
-        held_here, _, landed, cols = travels(c)
-        return remote(
-            held_here.at[block(d), cols],
-            landed.at[block(d), cols],
-            l_send.at[c, d],
-            l_recv.at[c, d],
-            me - QUAD,
-        )
+        here = partial.at[block(d), span(c)]
+        there = from_right.at[block(d), span(c)]
+        send, recv = l_send.at[sent_of(c, d)], l_recv.at[spot_of(c, d)]
+        return remote(here, there, send, recv, me - QUAD)
 
     def added(c, d, way):
         (right, left)[way](c, d).wait_recv()
-        landed, cols = travels(c)[1 + way], travels(c)[3]
-        return partial[block(d), span(c)] + landed[block(d), cols].astype(jnp.float32)
+        landed = (from_left, from_right)[way]
+        return partial[block(d), span(c)] + landed[block(d), span(c)]
 
     def pass_on(c, d, way):
-        to, cols = travels(c)[0], travels(c)[3]
-        to[block(d), cols] = added(c, d, way).astype(to.dtype)
+        partial[block(d), span(c)] = added(c, d, way)
         (right, left)[way](c, d).start()
 
     def sends(c, way):
@@ -451,7 +465,7 @@
         which, start, size = chunks[c]
         got = query.at[j, :, pl.ds(start, size)]
         to = (base + j) * QUAD + quad
-        return remote(got, got, q_send.at[c - lead, j], q_recv.at[c - lead], to)
+        return remote(got, got, q_send.at[0], q_recv.at[c - lead], to)
 
     def finish(c):
         if c == last:
@@ -489,7 +503,8 @@
     def tokens_ready(c, k):
         if c == 0 and share == 2:
             for step in near:
-                m_copy(step, k).wait_recv()
+                for piece_at in range(cuts):
+                    m_copy(step, k * cuts + piece_at).wait_recv()
 
     def project(c):
         which, start, size = chunks[c]
@@ -514,8 +529,6 @@
                 preferred_element_type=jnp.float32,
             )
         partial[:, span(c)] = total
-        if which == 2:
-            outgoing[:, cols] = total.astype(jnp.bfloat16)
         first_sends(c)
 
     def kv_rows(spot, of_side=False):
@@ -525,38 +538,40 @@
     def z_copy(way, j):
         got = kv_rows(j + way * half)
         to = me - QUAD if way else me + QUAD
-        return remote(got, got, z_send.at[way, j], z_recv.at[way, j], to)
+        return remote(got, got, z_send.at[way], z_recv.at[way, j], to)
 
     def y_copy(spot):
         got = kv_rows(spot)
-        return remote(got, got, y_send.at[spot], y_recv.at[spot], side)
+        return remote(got, got, y_send.at[0], y_recv.at[spot], side)
 
     def y_arrival(spot):
         got = kv_rows(spot, True)
-        return remote(got, got, y_send.at[spot], y_recv.at[spot], side)
+        return remote(got, got, y_send.at[0], y_recv.at[spot], side)
 
     def s_copy(spot, of_side):
         got = kv_rows(spot, of_side)
-        slot = spot + (line if of_side else 0)
-        return remote(got, got, s_send.at[slot], s_recv.at[slot], sib)
-
-    def s_arrival(spot, of_side):
-        at = lax.rem(side_sib if of_side else sib, QUAD)
-        got = cache.at[rows_of(spot * QUAD + at)]
-        slot = spot + (line if of_side else 0)
-        return remote(got, got, s_send.at[slot], s_recv.at[slot], sib)
-
-    def kv_pass(way, fresh):
+        return remote(got, got, s_send.at[0], s_recv.at[0], sib)
+
+    def s_all():
+        every = cache.at[pl.ds(0, 2 * line * tok_dev)]
+        return remote(every, every, s_send.at[0], s_recv.at[0], sib)
+
+    def kv_block(way, j, fresh):
+        if not fresh:
+            z_copy(way, j).wait_recv()
+
+        @pl.when(place > 0 if way else place < line - 1)
+        def _():
+            z_copy(way, j).start()
+
+        y_copy(j + way * half).start()
+        s_copy(j + way * half, False).start()
+
+    def kv_pass(way, fresh, near=None):
         def go(j, carry):
-            if not fresh:
-                z_copy(way, j).wait_recv()
-
-            @pl.when(place > 0 if way else place < line - 1)
-            def _():
-                z_copy(way, j).start()
-
-            y_copy(j + way * half).start()
-            s_copy(j + way * half, False).start()
+            kv_block(way, j, fresh)
+            if near is not None:
+                onward(near, j, 1 - way)
             return carry
 
         lax.fori_loop(0, half, go, 0)
@@ -576,12 +591,12 @@
             def _():
                 kv_pass(way, False)
 
-    def kv_far():
+    def kv_far(near):
         for way in range(2):
 
             @pl.when(2 * place < line if way else 2 * place >= line)
             def _():
-                kv_pass(way, False)
+                kv_pass(way, False, near)
 
     def kv_side():
         def go(spot, carry):
@@ -592,12 +607,7 @@
         lax.fori_loop(0, line, go, 0)
 
     def kv_ready():
-        def go(spot, carry):
-            s_arrival(spot, False).wait_recv()
-            s_arrival(spot, True).wait_recv()
-            return carry
-
-        lax.fori_loop(0, line, go, 0)
+        s_all().wait_recv()
 
     def mask():
         d_all().wait()
@@ -669,8 +679,7 @@
         return remote(every, every, o_send.at[0], o_recv.at[0], sib)
 
     def smooth():
-        for kind in range(3):
-            p_copy(kind).wait()
+        remote(theirs, theirs, p_send.at[0], p_recv.at[0], sib).wait()
         peak = jnp.maximum(
             jnp.maximum(mine[...], theirs[0]), jnp.maximum(theirs[1], theirs[2])
         )
@@ -681,13 +690,7 @@
             channel[0, here] = as_column(mine[:, at])
             at = pl.ds(pl.multiple_of(me * rows + i * LANES, LANES), LANES)
             channel[1, here] = as_column(gain_ref[:, at])
-        for which in range(3):
-            for step in range(tp_count):
-                if step == 0:
-                    x_copy(which, 0).wait()
-                else:
-                    x_copy(which, step).wait_send()
-                    x_copy(which, step).wait_recv()
+        x_all()
         relaid_out.start()
         tiles = relaid.shape[1] // LANES
 
@@ -732,8 +735,8 @@
         return remote(
             column.at[0],
             column_tp.at[step],
-            c_send.at[step],
-            c_recv.at[step],
+            c_send.at[0],
+            c_recv.at[0],
             me,
             lax.rem(tp + step, tp_count),
         )
@@ -751,15 +754,17 @@
         return remote(
             column.at[3],
             column_line.at[step],
-            a_send.at[step],
-            a_recv.at[step],
+            a_send.at[0],
+            a_recv.at[0],
             lax.rem(place + step, line) * QUAD + quad,
         )
 
     def columns_tp():
         joined = column[0]
+        if tp_count > 1:
+            every = column_tp.at[pl.ds(0, tp_count - 1)]
+            remote(every, every, c_send.at[0], c_recv.at[0], sib).wait()
         for step in range(1, tp_count):
-            c_copy(step).wait()
             joined = jnp.maximum(joined, column_tp[step])
         column[1] = joined
         b_copy(0).start()
@@ -777,8 +782,9 @@
 
     def columns_line():
         joined = column[3]
+        every = column_line.at[pl.ds(0, line - 1)]
+        remote(every, every, a_send.at[0], a_recv.at[0], sib).wait()
         for step in range(1, line):
-            a_copy(step).wait()
             joined = jnp.maximum(joined, column_line[step])
         scale_ref[...] = jnp.maximum(joined, 1e-05) / 127.0
 
@@ -810,33 +816,40 @@
 
     once(project, 0)
     early()
+    for which in (1, 2, 0):
+        for step in range(tp_count):
+            x_copy(which, step).start()
     for c in range(1, lead):
         once(project, c)
     for c in range(lead):
         pair(c - 1 if c else FAR, c)
     once(project, lead)
+    once(finish, kv_chunks[0])
     pair(lead - 1, lead)
+    once(project, lead + 1)
     for c in kv_chunks:
         once(finish, c)
     kv_start()
     mask()
-    once(project, lead + 1)
-    pair(lead, FAR)
-    kv_near()
+    pair(lead, lead + 1)
     smooth()
     once(project, lead + 2)
-    if lead + 3 <= last:
-        split_project(lead + 3, True)
-    kv_far()
-    pair(FAR, lead + 1)
     if lead < last - 1:
         once(finish, lead)
     if lead + 3 <= last:
+        split_project(lead + 3, True)
+    pair(lead + 1, FAR)
+    if lead + 1 < last - 1:
+        once(finish, lead + 1)
+    kv_near()
+    if lead + 3 <= last:
         split_project(lead + 3, False)
         ran.add((project, lead + 3))
-    pair(lead + 1, lead + 2)
-    if lead + 1 < last - 1:
-        once(finish, lead + 1)
+    if lead + 2 < last:
+        ran.add(("near", lead + 2))
+        kv_far(lead + 2)
+    else:
+        kv_far(None)
     columns_tp()
     for c in range(lead, count):
         once(project, c)
@@ -846,70 +859,63 @@
     kv_side()
     columns_side()
     kv_ready()
+    swap = last - 1 > lead
+
+    def attend_where(g, ends):
+        @pl.when(at_end if ends else jnp.logical_not(at_end))
+        def _():
+            attend(g)
+
     for c in range(lead, count):
         once(finish, c)
-        attend(c - lead)
+        if swap and c == last - 1:
+            attend_where(c - lead, True)
+        else:
+            attend(c - lead)
+    if swap:
+        attend_where(last - 1 - lead, False)
     columns_line()
     o_all().wait()
     out_peak_ref[...] = jnp.max(out_all[...], axis=0)
 
-    for step in range(1, line):
-        for k in range(QUAD):
-            t_copy(step, k).wait_send()
-            if share == 2:
-                m_copy(step, k).wait_send()
-    for c in range(count):
-        for kind in range(3):
-            w_copy(kind, c).wait_send()
+    tokens_sent(t_send.at[0])
+    if share == 2:
+        tokens_sent(m_send.at[0])
+    for which in range(3):
+        every = held[which]
+        remote(every, every, w_send.at[which], w_send.at[which], sib).wait_send()
+    for way in range(2):
+        moves = place > 0 if way else place < line - 1
+
+        @pl.when(moves)
+        def _():
+            sems = (r_send, l_send)[way]
+            for c in range(last):
+                every = partial.at[pl.ds(0, half * tok_dev), span(c)]
+                remote(every, every, sems.at[c], sems.at[c], sib).wait_send()
+            every = cache.at[pl.ds(0, half * tok_dev)]
+            remote(every, every, z_send.at[way], z_send.at[way], sib).wait_send()
 
         def sent(d, carry):
-            if c < last:
-                to_right, to_left = d >= half, d < half
-            else:
-                to_right, to_left = d > place, d < place
-
-            @pl.when(to_right & (place < line - 1))
+            @pl.when(d < place if way else d > place)
             def _():
-                right(c, d).wait_send()
-
-            @pl.when(to_left & (place > 0))
-            def _():
-                left(c, d).wait_send()
+                (right, left)[way](last, d).wait_send()
 
             return carry
 
         lax.fori_loop(0, line, sent, 0)
-
-    for c in range(lead, last):
+    if last > lead and half > 1:
 
         @pl.when(at_end)
         def _():
-            def q_sent(j, carry):
-                @pl.when(base + j != place)
-                def _():
-                    q_copy(c, j).wait_send()
-
-                return carry
-
-            lax.fori_loop(0, half, q_sent, 0)
-
-    def kv_sent(spot, carry):
-        y_copy(spot).wait_send()
-        s_copy(spot, False).wait_send()
-        s_copy(spot, True).wait_send()
-        return carry
-
-    lax.fori_loop(0, line, kv_sent, 0)
-    for way in range(2):
-
-        @pl.when(place > 0 if way else place < line - 1)
-        def _():
-            def z_sent(j, carry):
-                z_copy(way, j).wait_send()
-                return carry
-
-            lax.fori_loop(0, half, z_sent, 0)
-
+            every = query.at[
+                pl.ds(0, half - 1), :, pl.ds(0, (last - lead) * GROUP * HEAD)
+            ]
+            remote(every, every, q_send.at[0], q_send.at[0], sib).wait_send()
+
+    s_all().wait_send()
+    every = cache.at[pl.ds(0, line * tok_dev)]
+    remote(every, every, y_send.at[0], y_send.at[0], sib).wait_send()
     relaid_out.wait()
 
 
@@ -939,7 +945,7 @@
             jax.ShapeDtypeStruct((sub, LANES), f32),
             jax.ShapeDtypeStruct((sub, total * tp_count), bf16),
         ),
-        in_specs=[vmem] * 6,
+        in_specs=[vmem] * 3 + [pl.BlockSpec(memory_space=pl.ANY)] * 3,
         out_specs=(vmem,) * 5 + (pl.BlockSpec(memory_space=pl.ANY),),
         scratch_shapes=[
             pltpu.VMEM((tok_dev, depth), bf16),
@@ -953,9 +959,9 @@
             pltpu.VMEM((1, QUAD * rows), f32),
             pltpu.VMEM((3, 1, QUAD * rows), f32),
         ]
+        + [pltpu.VMEM((rows, width), bf16) for width in widths]
         + [pltpu.VMEM((3, rows, width), bf16) for width in widths]
         + [pltpu.VMEM((line * tok_dev, total), f32)] * 3
-        + [pltpu.VMEM((line * tok_dev, widths[2]), bf16)] * 3
         + [
             pltpu.VMEM((line // 2, tok_dev, widths[0]), bf16),
             pltpu.VMEM((tok_dev * tok_count, widths[1] + widths[2]), bf16),
@@ -967,21 +973,19 @@
             pltpu.VMEM((1, widths[0]), f32),
             pltpu.VMEM((tok_count, 1, widths[0]), f32),
         ]
-        + [dma((3, count))] * 2
-        + [dma((line, QUAD))] * 4
-        + [dma((3, tp_count))] * 2
-        + [dma((4,))]
-        + [dma((count, line))] * 4
-        + [dma((3,))] * 2
+        + [dma((3,)), dma((3,)), dma((3, count))]
+        + [dma((1,)), dma((line, 2 * QUAD))] * 2
         + [dma((1,))] * 2
-        + [dma((2, line // 2))] * 2
-        + [dma((line,))] * 2
-        + [dma((2 * line,))] * 2
-        + [dma((queries, line // 2)), dma((queries,))]
-        + [dma((tp_count,))] * 2
+        + [dma((2,))]
+        + [dma((count - 1 + line,)), dma(((count - 1) * (line // 2) + line,))] * 2
+        + [dma((1,))] * 4
+        + [dma((2,)), dma((2, line // 2))]
+        + [dma((1,)), dma((line,))]
+        + [dma((1,))] * 2
+        + [dma((1,)), dma((queries,))]
+        + [dma((1,))] * 2
         + [dma((2,))] * 2
-        + [dma((line,))] * 2
-        + [dma((1,))] * 2,
+        + [dma((1,))] * 4,
         compiler_params=pltpu.CompilerParams(
             collective_id=0, has_side_effects=True, vmem_limit_bytes=63 * 1024 * 1024
         ),

time: 123 us -> 120 us (0.976)
  Pallas kernels: 122 us -> 119 us
    pallas_call x1, Pallas kernels: 118 us -> 114 us  [calibrate(): pl.pallas_call(functools.partial(main_kernel, chunks, line, tp_count, sha...]
where the time goes in v4:
time: 120 us; the launch traced here: 119 us
  Pallas kernels  119 us (99%)
    pallas_call x1, Pallas kernels, calibrate(): pl.pallas_call(functools.partial(main_kernel, chunks, line, tp_count, sha...  114 us
    pallas_call x1, Pallas kernels, coded(): pl.pallas_call(functools.partial(codes_kernel, widths, tp_count), grid=(s...  4.59 us

profile of v4, /device:TPU:0, one launch (start us, length us, event | category | flops | bytes accessed | tf_op | source)
XLA Modules:
  0.0 119.5 jit_solution(9763620878288073915)
XLA Ops:
  0.6 114.2 %shard_map.133 = (bf16[96,2048]{1,0:T(8,128)(2,1)}, f32[1,2048]{1,0:T(1,128)}, f32[1,6144]{1,0:T(1,128)}, f32[1,256]{1,0:T(1,128)}, f32[256,128]{1,0:T(8,128)}, /*index=5*/bf16[256,6144]{1,0:T(8,128)(2,1)}) custom-call(bf16[96,8192]{1,0:T(8,128)(2,1)} %hidden_ref.1, f32[1,8192]{1,0:T(1,128)} %bitcast.7, s32[1,96]{1,0:T(1,128)} %bitcast.8, ...), custom_call_target="tpu_custom_call" | custom-call | tf_op jit(solution)/shard_map/pallas_call | solution.py:938
  114.8 4.6 %shard_map.134 = (f32[256,4096]{1,0:T(8,128)}, f32[256,1024]{1,0:T(8,128)}, f32[256,1024]{1,0:T(8,128)}, f32[1,2048]{1,0:T(1,128)}, f32[1,512]{1,0:T(1,128)}, /*...) custom-call(bf16[256,6144]{1,0:T(8,128)(2,1)} %get-tuple-element.24.relaid_ref, ...), custom_call_target="tpu_custom_call" | custom-call | tf_op jit(solution)/shard_map/pallas_call | solution.py:1054

commit v5 on v4

--- a/solution.py
+++ b/solution.py
@@ -35,9 +35,9 @@
     line,
     tp_count,
     share,
-    hidden_ref,
-    gain_ref,
-    doc_ref,
+    hidden_from,
+    gain_from,
+    doc_from,
     wq_from,
     wk_from,
     wv_from,
@@ -57,6 +57,9 @@
     tokens,
     mine,
     theirs,
+    hidden_ref,
+    gain_ref,
+    doc_ref,
     wq_ref,
     wk_ref,
     wv_ref,
@@ -221,7 +224,7 @@
         source = lax.rem(place - step + line, line)
         start = pl.multiple_of(source * tok_dev + piece * part, 16)
         got = tokens.at[pl.ds(start, part), pl.ds(channels(k), slab)]
-        return remote(got, got, m_send.at[0], m_recv.at[step, k], me, mate)
+        return remote(got, got, m_send.at[0], m_recv.at[k], me, mate)
 
     def tokens_sent(sem):
         every = tokens.at[pl.ds(0, (line - 1) * part)]
@@ -286,14 +289,24 @@
 
         lax.fori_loop(0, reach // (tiles_at * LANES), go, 0)
 
+    arrays = (
+        (hidden_from, hidden_ref),
+        (gain_from, gain_ref),
+        (doc_from, doc_ref),
+        (wk_from, wk_ref),
+        (wv_from, wv_ref),
+        (wq_from, wq_ref),
+    )
     loads = [
-        pltpu.make_async_copy(source, own[which], w_local.at[which])
-        for which, source in enumerate((wq_from, wk_from, wv_from))
+        pltpu.make_async_copy(source, target, w_local.at[at])
+        for at, (source, target) in enumerate(arrays)
     ]
-    for which in (1, 2, 0):
-        loads[which].start()
+    for load in loads:
+        load.start()
     barrier = pltpu.get_barrier_semaphore()
     meet(barrier)
+    for load in loads[:3]:
+        load.wait()
     doc_row[...] = jnp.full(doc_row.shape, FAR, jnp.int32)
     doc_row[:, :tok_dev] = doc_ref[...]
     docs[me] = doc_row[...]
@@ -313,7 +326,7 @@
     pl.semaphore_wait(barrier, tok_count - 1 + tp_count - 1)
 
     each(d_copy)
-    for load in loads:
+    for load in loads[3:]:
         load.wait()
     for c in range(min(ahead, count)):
         weights_start(c)
@@ -344,12 +357,27 @@
         return carry
 
     lax.fori_loop(0, half, tables, 0)
-    near = sorted(range(1, line), key=lambda step: min(step, line - step))
-    for k in range(QUAD * cuts):
-        for step in near:
+    def take_tokens(i, k):
+        source = jnp.where(i < half, i, line - 1 - (i - half))
+        source = jnp.where(2 * place < line, source, line - 1 - source)
+
+        @pl.when(source != place)
+        def _():
+            step = lax.rem(place - source + line, line)
             t_copy(step, k).wait_recv()
             if share == 2:
                 m_copy(step, k).start()
+
+    for k in range(QUAD * cuts):
+
+        def take(i, carry):
+            take_tokens(i, k)
+            return carry
+
+        lax.fori_loop(0, line - 1, take, 0)
+    for k in range(QUAD * cuts):
+        take_tokens(line - 1, k)
+
     base_of = [sum(size for _, _, size in chunks[:c]) for c in range(count)]
 
     def span(c):
@@ -502,9 +530,9 @@
 
     def tokens_ready(c, k):
         if c == 0 and share == 2:
-            for step in near:
-                for piece_at in range(cuts):
-                    m_copy(step, k * cuts + piece_at).wait_recv()
+            for at in range(k * cuts, (k + 1) * cuts):
+                every = tokens.at[pl.ds(0, (line - 1) * part), pl.ds(0, slab)]
+                remote(every, every, m_recv.at[at], m_recv.at[at], sib).wait_recv()
 
     def project(c):
         which, start, size = chunks[c]
@@ -854,11 +882,11 @@
     for c in range(lead, count):
         once(project, c)
         pair(c - 1, c)
+    kv_side()
     columns_sib()
-    pair(last, FAR)
-    kv_side()
-    columns_side()
     kv_ready()
+    if lead == last:
+        pair(last, FAR)
     swap = last - 1 > lead
 
     def attend_where(g, ends):
@@ -867,11 +895,16 @@
             attend(g)
 
     for c in range(lead, count):
+        if lead < c == last - 2:
+            once(finish, last - 1)
         once(finish, c)
         if swap and c == last - 1:
             attend_where(c - lead, True)
         else:
             attend(c - lead)
+        if c == lead:
+            pair(last, FAR)
+            columns_side()
     if swap:
         attend_where(last - 1 - lead, False)
     columns_line()
@@ -945,7 +978,7 @@
             jax.ShapeDtypeStruct((sub, LANES), f32),
             jax.ShapeDtypeStruct((sub, total * tp_count), bf16),
         ),
-        in_specs=[vmem] * 3 + [pl.BlockSpec(memory_space=pl.ANY)] * 3,
+        in_specs=[pl.BlockSpec(memory_space=pl.ANY)] * 6,
         out_specs=(vmem,) * 5 + (pl.BlockSpec(memory_space=pl.ANY),),
         scratch_shapes=[
             pltpu.VMEM((tok_dev, depth), bf16),
@@ -959,6 +992,7 @@
             pltpu.VMEM((1, QUAD * rows), f32),
             pltpu.VMEM((3, 1, QUAD * rows), f32),
         ]
+        + [pltpu.VMEM(array.shape, array.dtype) for array in (hidden, gain, doc_row)]
         + [pltpu.VMEM((rows, width), bf16) for width in widths]
         + [pltpu.VMEM((3, rows, width), bf16) for width in widths]
         + [pltpu.VMEM((line * tok_dev, total), f32)] * 3
@@ -973,8 +1007,8 @@
             pltpu.VMEM((1, widths[0]), f32),
             pltpu.VMEM((tok_count, 1, widths[0]), f32),
         ]
-        + [dma((3,)), dma((3,)), dma((3, count))]
-        + [dma((1,)), dma((line, 2 * QUAD))] * 2
+        + [dma((6,)), dma((3,)), dma((3, count))]
+        + [dma((1,)), dma((line, 2 * QUAD)), dma((1,)), dma((2 * QUAD,))]
         + [dma((1,))] * 2
         + [dma((2,))]
         + [dma((count - 1 + line,)), dma(((count - 1) * (line // 2) + line,))] * 2

time: 120 us -> 118 us (0.983)
  Pallas kernels: 119 us -> 117 us
    pallas_call x1, Pallas kernels: 114 us -> 113 us  [calibrate(): pl.pallas_call(functools.partial(main_kernel, chunks, line, tp_count, sha...]
where the time goes in v5:
time: 118 us
  Pallas kernels  117 us (99%)
    pallas_call x1, Pallas kernels, calibrate(): pl.pallas_call(functools.partial(main_kernel, chunks, line, tp_count, sha...  113 us
    pallas_call x1, Pallas kernels, coded(): pl.pallas_call(functools.partial(codes_kernel, widths, tp_count), grid=(s...  4.59 us

profile of v5, /device:TPU:0, one launch (start us, length us, event | category | flops | bytes accessed | tf_op | source)
XLA Modules:
  0.0 118.1 jit_solution(18288467220703866643)
XLA Ops:
  0.6 112.8 %shard_map.133 = (bf16[96,2048]{1,0:T(8,128)(2,1)}, f32[1,2048]{1,0:T(1,128)}, f32[1,6144]{1,0:T(1,128)}, f32[1,256]{1,0:T(1,128)}, f32[256,128]{1,0:T(8,128)}, /*index=5*/bf16[256,6144]{1,0:T(8,128)(2,1)}) custom-call(bf16[96,8192]{1,0:T(8,128)(2,1)} %hidden_from.1, f32[1,8192]{1,0:T(1,128)} %bitcast.7, s32[1,96]{1,0:T(1,128)} %bitcast.8, ...), custom_call_target="tpu_custom_call" | custom-call | tf_op jit(solution)/shard_map/pallas_call | solution.py:971
  113.4 4.6 %shard_map.134 = (f32[256,4096]{1,0:T(8,128)}, f32[256,1024]{1,0:T(8,128)}, f32[256,1024]{1,0:T(8,128)}, f32[1,2048]{1,0:T(1,128)}, f32[1,512]{1,0:T(1,128)}, /*...) custom-call(bf16[256,6144]{1,0:T(8,128)(2,1)} %get-tuple-element.24.relaid_ref, ...), custom_call_target="tpu_custom_call" | custom-call | tf_op jit(solution)/shard_map/pallas_call | solution.py:1088

commit v6 on v5

--- a/solution.py
+++ b/solution.py
@@ -425,18 +425,22 @@
             return place < line - 1 if way == 0 else place > 0
         return d > place if way == 0 else d < place
 
-    def first_sends(c):
-        for way in range(2):
-
-            @pl.when(place == (0 if way == 0 else line - 1))
-            def _():
-                size, pick = sends(c, way)
-
-                def go(i, carry):
-                    (right, left)[way](c, pick(i)).start()
-                    return carry
-
-                lax.fori_loop(0, size, go, 0)
+    def first_sends(c, between):
+        for stage in range(2):
+            for way in range(2):
+
+                @pl.when(place == (0 if way == 0 else line - 1))
+                def _():
+                    size, pick = sends(c, way)
+
+                    def go(i, carry):
+                        (right, left)[way](c, pick(i)).start()
+                        return carry
+
+                    lax.fori_loop(stage, size if stage else 1, go, 0)
+
+            if stage == 0 and between is not None:
+                between()
 
     def onward(c, i, way):
         size, pick = sends(c, way)
@@ -534,7 +538,7 @@
                 every = tokens.at[pl.ds(0, (line - 1) * part), pl.ds(0, slab)]
                 remote(every, every, m_recv.at[at], m_recv.at[at], sib).wait_recv()
 
-    def project(c):
+    def project(c, between=None):
         which, start, size = chunks[c]
         cols = slice(start, start + size)
         tokens_ready(c, 0)
@@ -557,7 +561,7 @@
                 preferred_element_type=jnp.float32,
             )
         partial[:, span(c)] = total
-        first_sends(c)
+        first_sends(c, between)
 
     def kv_rows(spot, of_side=False):
         at = lax.rem(side, QUAD) if of_side else quad
@@ -668,29 +672,37 @@
             def _():
                 q_copy(g + lead, place - base).wait_recv()
 
-        asked = jnp.concatenate(
-            [query[place - base, :, head] for head in heads], axis=0
-        )
         key = cache[:, g * HEAD : (g + 1) * HEAD]
         value = cache[:, (kv_here + g) * HEAD : (kv_here + g + 1) * HEAD]
-        scores = lax.dot_general(
-            asked, key, (((1,), (1,)), ((), ())), preferred_element_type=jnp.float32
-        )
-        scores = (
-            scores.reshape(GROUP, tok_dev, keys) + bias[...][None]
-        ).reshape(GROUP * tok_dev, keys)
-        weights = jnp.exp2((scores - jnp.max(scores, axis=1, keepdims=True)) * turn)
-        totals = jnp.sum(weights, axis=1, keepdims=True)
-        mixed = jnp.dot(
-            weights.astype(jnp.bfloat16), value, preferred_element_type=jnp.float32
-        )
-        mixed = (mixed / totals).astype(jnp.bfloat16)
-        for h, head in enumerate(heads):
-            piece = mixed[h * tok_dev : (h + 1) * tok_dev]
-            out_ref[:, head] = piece
-            out_mine[:, head] = jnp.max(
-                jnp.abs(piece.astype(jnp.float32)), axis=0, keepdims=True
+
+        def scored(some):
+            asked = jnp.concatenate(
+                [query[place - base, :, head] for head in some], axis=0
             )
+            scores = lax.dot_general(
+                asked, key, (((1,), (1,)), ((), ())), preferred_element_type=jnp.float32
+            )
+            scores = scores.reshape(len(some), tok_dev, keys) + bias[...][None]
+            return scores.reshape(len(some) * tok_dev, keys)
+
+        def mixed_of(some, scores):
+            weights = jnp.exp2((scores - jnp.max(scores, axis=1, keepdims=True)) * turn)
+            totals = jnp.sum(weights, axis=1, keepdims=True)
+            mixed = jnp.dot(
+                weights.astype(jnp.bfloat16), value, preferred_element_type=jnp.float32
+            )
+            mixed = (mixed / totals).astype(jnp.bfloat16)
+            for h, head in enumerate(some):
+                piece = mixed[h * tok_dev : (h + 1) * tok_dev]
+                out_ref[:, head] = piece
+                out_mine[:, head] = jnp.max(
+                    jnp.abs(piece.astype(jnp.float32)), axis=0, keepdims=True
+                )
+
+        pairs = [heads[: GROUP // 2], heads[GROUP // 2 :]]
+        held_scores = [scored(some) for some in pairs]
+        for some, scores in zip(pairs, held_scores):
+            mixed_of(some, scores)
         cols = pl.ds(g * GROUP * HEAD, GROUP * HEAD)
         out_all[me, :, cols] = out_mine[:, cols]
         each(functools.partial(o_copy, g))
@@ -837,10 +849,10 @@
         if far is not None or near is not None:
             weave(far, near)
 
-    def split_project(c, ends):
+    def split_project(c, ends, between=None):
         @pl.when(at_end if ends else jnp.logical_not(at_end))
         def _():
-            project(c)
+            project(c, between)
 
     once(project, 0)
     early()
@@ -862,10 +874,11 @@
     pair(lead, lead + 1)
     smooth()
     once(project, lead + 2)
-    if lead < last - 1:
-        once(finish, lead)
+    due = functools.partial(once, finish, lead) if lead < last - 1 else None
     if lead + 3 <= last:
-        split_project(lead + 3, True)
+        split_project(lead + 3, True, due)
+    elif due is not None:
+        due()
     pair(lead + 1, FAR)
     if lead + 1 < last - 1:
         once(finish, lead + 1)

time: 118 us -> 118 us (level)
  no operation moved by 1% of the time
where the time goes in v6:
time: 118 us; the launch traced here: 117 us
  Pallas kernels  117 us (99%)
    pallas_call x1, Pallas kernels, calibrate(): pl.pallas_call(functools.partial(main_kernel, chunks, line, tp_count, sha...  112 us
    pallas_call x1, Pallas kernels, coded(): pl.pallas_call(functools.partial(codes_kernel, widths, tp_count), grid=(s...  4.59 us

profile of v6, /device:TPU:0, one launch (start us, length us, event | category | flops | bytes accessed | tf_op | source)
XLA Modules:
  0.0 117.5 jit_solution(9779695870555168476)
XLA Ops:
  0.6 112.2 %shard_map.133 = (bf16[96,2048]{1,0:T(8,128)(2,1)}, f32[1,2048]{1,0:T(1,128)}, f32[1,6144]{1,0:T(1,128)}, f32[1,256]{1,0:T(1,128)}, f32[256,128]{1,0:T(8,128)}, /*index=5*/bf16[256,6144]{1,0:T(8,128)(2,1)}) custom-call(bf16[96,8192]{1,0:T(8,128)(2,1)} %hidden_from.1, f32[1,8192]{1,0:T(1,128)} %bitcast.7, s32[1,96]{1,0:T(1,128)} %bitcast.8, ...), custom_call_target="tpu_custom_call" | custom-call | tf_op jit(solution)/shard_map/pallas_call | solution.py:984
  112.8 4.6 %shard_map.134 = (f32[256,4096]{1,0:T(8,128)}, f32[256,1024]{1,0:T(8,128)}, f32[256,1024]{1,0:T(8,128)}, f32[1,2048]{1,0:T(1,128)}, f32[1,512]{1,0:T(1,128)}, /*...) custom-call(bf16[256,6144]{1,0:T(8,128)(2,1)} %get-tuple-element.24.relaid_ref, ...), custom_call_target="tpu_custom_call" | custom-call | tf_op jit(solution)/shard_map/pallas_call | solution.py:1101
